TPU v7x, 128 devices: a whole 4x4x4 slice. The times are simulated.
128 devices in a mesh: gz: 2 (over x_hi), row: 8 (over y, core), col: 8 (over z, x_lo).
Axes of the slice: x: 4 (x_hi: 2, x_lo: 2; x = x_hi * 2 + x_lo), y: 4, z: 4, core: 2. Of those that a mesh axis runs over, the one named last changes fastest.
Arguments:
- sections: bfloat16 [4, 4096, 4096], P('gz', 'row', 'col'), may hold values from -6 to 6
- priors: int32 [2, 4, 16, 16], P(None, 'gz', 'row', 'col'), may hold values from -64 to 64
- row_order: int32 [16], replicated, may hold values from 0 to 15, each once
Outputs:
- mesh_flows: float32 [16, 128], P('row')
Inputs may be any that keep to these rules, and one draw needn't show every extreme that they name: A permutation of the patch rows: mesh row m holds patch row row_order[m].
All inputs are finite; a program needn't handle non-finite values.
Results may differ from a plain program's by a relative error of at most 0.0003.
Values may be sent and summed in bfloat16 or wider, within the bound.
A program may use at most 64 MiB of HBM per device.

v0:
```python
import math

import jax
import jax.numpy as jnp
from jax import lax
from jax.sharding import Mesh
from jax.sharding import PartitionSpec as P

PATCH = 512
STRIDE = 256
LAGS = 128
HALO = 256
ROW = ("row_0", "row_1")
COL = ("col_0", "col_1")
GZ_ROW_COL = ("gz", "row_0", "row_1", "col_0", "col_1")


def with_halo(shard, sides, width):
    for axis, dim in sides:
        devices, length = (lax.axis_size(axis), shard.shape[dim])
        up = [(i, (i + 1) % devices) for i in range(devices - 1)]
        down = [(j, i) for i, j in up]
        last = lax.slice_in_dim(shard, length - width, length, axis=dim)
        first = lax.slice_in_dim(shard, 0, width, axis=dim)
        before = lax.ppermute(last, axis, up)
        after = lax.ppermute(first, axis, down)
        shard = jnp.concatenate([before, shard, after], axis=dim)
    return shard


def shifted(value, axis, steps):
    count = lax.axis_size(axis)
    pairs = [(source, (source + steps) % count) for source in range(count)]
    return lax.ppermute(value, axis, pairs)


def cut_rows(length, count):
    turn = length // count
    if turn >= 8:
        turn -= turn % 8
    return [turn * k for k in range(1, count)]


def all_blocks(shard, axes, order):
    parts = shard
    for k in order:
        parts = lax.all_gather(parts, axes[k])
    done = order[::-1]
    back = [done.index(k) for k in range(len(axes))]
    parts = parts.transpose(*back, *range(len(axes), parts.ndim))
    return parts.reshape(-1, *shard.shape)


def joined_along(parts, dim):
    shape = list(parts.shape[1:])
    shape[dim] *= parts.shape[0]
    return jnp.moveaxis(parts, 0, dim).reshape(shape)


def spread_gather(shard, axes, dim):
    numbers = list(range(len(axes)))[::-1]
    split_at = shard.shape.index(max(shard.shape[:-1] or shard.shape))
    edges = [0, *cut_rows(shard.shape[split_at], len(axes)), shard.shape[split_at]]
    finished = []
    for k, (start, end) in enumerate(zip(edges, edges[1:])):
        if end > start:
            piece = lax.slice_in_dim(shard, start, end, axis=split_at)
            finished.append(all_blocks(piece, axes, numbers[k:] + numbers[:k]))
    return joined_along(jnp.concatenate(finished, axis=split_at + 1), dim)


def dft_tables(length):
    frequencies = jnp.arange(length, dtype=jnp.int32)
    angles = jnp.mod(frequencies[:, None] * frequencies[None, :], length).astype(jnp.float32) * (
        2.0 * math.pi / length
    )
    cosine = jnp.cos(angles)
    sine_part = jnp.sin(angles)
    minus_table = jnp.concatenate([cosine, -sine_part], axis=1).astype(jnp.bfloat16)
    plus_table = jnp.concatenate([cosine, sine_part], axis=1).astype(jnp.bfloat16)
    return (minus_table, plus_table)


def spectra_of(patches, minus_table, plus_table):
    length = patches.shape[-1]
    row_pass = jnp.einsum(
        "nxy,yk->nxk", patches, minus_table, preferred_element_type=jnp.float32
    ).astype(jnp.bfloat16)
    real_rows = row_pass[:, :, :length]
    imag_rows = row_pass[:, :, length:]
    upper_stack = jnp.concatenate([real_rows, imag_rows], axis=1)
    lower_stack = jnp.concatenate([imag_rows, real_rows], axis=1)
    spec_real = (
        jnp.einsum("kx,nxm->nkm", plus_table, upper_stack, preferred_element_type=jnp.float32)
        / length
    )
    spec_imag = (
        jnp.einsum("kx,nxm->nkm", minus_table, lower_stack, preferred_element_type=jnp.float32)
        / length
    )
    return jnp.stack([spec_real, spec_imag], axis=1).astype(jnp.bfloat16)


def lag_angles(offsets, length):
    frequencies = jnp.arange(length, dtype=jnp.int32)
    shifts = offsets[:, None] + jnp.arange(LAGS, dtype=jnp.int32)[None, :] - LAGS // 2
    angles = jnp.mod(shifts[:, :, None] * frequencies[None, None, :], length).astype(
        jnp.float32
    ) * (2.0 * math.pi / length)
    return (jnp.cos(angles), jnp.sin(angles))


def flows_of(first_spec, second_spec, offsets):
    length = first_spec.shape[-1]
    first_real = first_spec[:, 0].astype(jnp.float32)
    first_imag = first_spec[:, 1].astype(jnp.float32)
    second_real = second_spec[:, 0].astype(jnp.float32)
    second_imag = second_spec[:, 1].astype(jnp.float32)
    prod_real = (first_real * second_real + first_imag * second_imag).astype(jnp.bfloat16)
    prod_imag = (first_real * second_imag - first_imag * second_real).astype(jnp.bfloat16)
    row_cosine, row_sine = lag_angles(offsets[0], length)
    column_cosine, column_sine = lag_angles(offsets[1], length)
    products = jnp.concatenate([prod_real, prod_imag], axis=2)
    column_real = jnp.concatenate([column_cosine, -column_sine], axis=2).astype(jnp.bfloat16)
    column_imag = jnp.concatenate([column_sine, column_cosine], axis=2).astype(jnp.bfloat16)
    half_real = jnp.einsum(
        "nkl,nul->nku", products, column_real, preferred_element_type=jnp.float32
    ).astype(jnp.bfloat16)
    half_imag = jnp.einsum(
        "nkl,nul->nku", products, column_imag, preferred_element_type=jnp.float32
    ).astype(jnp.bfloat16)
    row_table = jnp.concatenate([row_cosine, -row_sine], axis=2).astype(jnp.bfloat16)
    stacked = jnp.concatenate([half_real, half_imag], axis=1)
    surface = (
        jnp.einsum("ntk,nku->ntu", row_table, stacked, preferred_element_type=jnp.float32) / length
    )
    weights = surface * surface
    displacement = (jnp.arange(LAGS, dtype=jnp.int32) - LAGS // 2).astype(jnp.float32)
    weight_sum = 1.0 + jnp.sum(weights, axis=(1, 2))
    row_shift = jnp.sum(weights * displacement[None, :, None], axis=(1, 2)) / weight_sum
    column_shift = jnp.sum(weights * displacement[None, None, :], axis=(1, 2)) / weight_sum
    return jnp.stack(
        [offsets[0].astype(jnp.float32) + row_shift, offsets[1].astype(jnp.float32) + column_shift],
        axis=0,
    )


def body(sections, priors, row_order):
    sec_count = sections.shape[0]
    block_side = sections.shape[1]
    per_side = block_side // STRIDE
    place_count = per_side * per_side
    margin = HALO // 2
    minus_table, plus_table = dft_tables(PATCH)
    offsets_all = jnp.transpose(priors, (2, 3, 0, 1)).reshape(place_count, 2, sec_count)
    positions = jnp.arange(place_count, dtype=jnp.int32)

    def cut_window(extended, position):
        top_edge = position // per_side * STRIDE
        left_edge = position % per_side * STRIDE
        return lax.dynamic_slice(
            extended, (jnp.int32(0), top_edge, left_edge), (extended.shape[0], PATCH, PATCH)
        )

    arrived = shifted(sections[:1], "gz", -1)
    extended = with_halo(jnp.concatenate([sections, arrived], axis=0), ((ROW, 1), (COL, 2)), margin)

    def place_flows(inputs):
        position, offsets = inputs
        section_spectra = spectra_of(cut_window(extended, position), minus_table, plus_table)
        return flows_of(section_spectra[:-1], section_spectra[1:], offsets)

    all_flows = lax.map(place_flows, (positions, offsets_all))
    local_table = jnp.transpose(all_flows.reshape(per_side, per_side, 2, sec_count), (2, 3, 0, 1))
    flat_flows = local_table.reshape(1, 2 * sec_count * place_count)
    gathered = spread_gather(flat_flows, GZ_ROW_COL, 0)
    size_gz = lax.axis_size("gz")
    size_row = lax.axis_size(ROW)
    size_col = lax.axis_size(COL)
    whole_grid = gathered.reshape(size_gz, size_row, size_col, 2, sec_count, per_side, per_side)
    whole_grid = jnp.transpose(whole_grid, (3, 0, 4, 1, 5, 2, 6)).reshape(
        2, size_gz * sec_count, size_row * per_side, size_col * per_side
    )
    rows_each = row_order.shape[0] // size_row
    owned = lax.dynamic_slice_in_dim(row_order, lax.axis_index(ROW) * rows_each, rows_each)
    selector = (owned[:, None] == jnp.arange(row_order.shape[0], dtype=jnp.int32)[None, :]).astype(
        jnp.float32
    )
    picked = jnp.einsum("jr,csrk->jcsk", selector, whole_grid, precision=lax.Precision.HIGHEST)
    return picked.reshape(rows_each, 2 * size_gz * sec_count * size_col * per_side)


def solution(mesh):
    torus = Mesh(
        mesh.devices.reshape(mesh.shape["gz"], 4, 2, 4, 2),
        ("gz", "row_0", "row_1", "col_0", "col_1"),
    )
    return jax.shard_map(
        body,
        mesh=torus,
        in_specs=(P("gz", ROW, COL), P(None, "gz", ROW, COL), P()),
        out_specs=P(ROW, None),
        check_vma=False,
    )
```

profile of v0, /device:TPU:1, one launch (start us, length us, event | category | flops | bytes accessed | tf_op | source)
XLA Modules:
  0.0 176.7 jit_solution(2236564331779916363)
XLA Ops:
  1.1 3.6 %collective-permute-start = (bf16[1,512,512]{2,1,0:T(8,128)(2,1)S(1)}, bf16[1,512,512]{2,1,0:T(8,128)(2,1)S(1)}, u32[]{:S(2)}, u32[]{:S(2)}) collective-permute-start(bf16[1,512,512]{2,1,0:T(8,128)(2,1)S(1)} %slice.97), channel_id=1, source_target_pairs={{0,64},{64,0},{1,65},{65,1},{2,66},{66,2},{3,67},{67,3},{4,68},{68... | collective-permute-start | bytes 1572872 | tf_op jit(solution)/shard_map/ppermute | solution.py:34
  6.0 9.9 %collective-permute-done = bf16[1,512,512]{2,1,0:T(8,128)(2,1)S(1)} collective-permute-done((bf16[1,512,512]{2,1,0:T(8,128)(2,1)S(1)}, bf16[1,512,512]{2,1,0:T(8,128)(2,1)S(1)}, u32[]{:S(2)}, u32[]{:S(2)}) %collective-permute-start) | collective-permute-done | bytes 524320 | tf_op jit(solution)/shard_map/ppermute | solution.py:34
  16.1 5.0 %collective-permute-start.1 = (bf16[3,128,512]{2,1,0:T(8,128)(2,1)S(1)}, bf16[3,128,512]{2,1,0:T(8,128)(2,1)S(1)}, u32[]{:S(2)}, u32[]{:S(2)}) collective-permute-start(bf16[3,128,512]{2,1,0:T(8,128)(2,1)S(1)} %get-tuple-element.196), channel_id=1, source_target_pairs={{0,8},{8,16},{16,24},{24,32},{32,40},{40,48},{48,56},{1,9},{9,17},... | collective-permute-start | bytes 1179656 | tf_op jit(solution)/shard_map/ppermute | solution.py:25
  21.0 1.9 %collective-permute-start.2 = (bf16[3,128,512]{2,1,0:T(8,128)(2,1)S(1)}, bf16[3,128,512]{2,1,0:T(8,128)(2,1)S(1)}, u32[]{:S(2)}, u32[]{:S(2)}) collective-permute-start(bf16[3,128,512]{2,1,0:T(8,128)(2,1)S(1)} %get-tuple-element.197), channel_id=1, source_target_pairs={{8,0},{16,8},{24,16},{32,24},{40,32},{48,40},{56,48},{9,1},{17,9},... | collective-permute-start | bytes 1179656 | tf_op jit(solution)/shard_map/ppermute | solution.py:26
  23.0 2.8 %collective-permute-done.1 = bf16[3,128,512]{2,1,0:T(8,128)(2,1)S(1)} collective-permute-done((bf16[3,128,512]{2,1,0:T(8,128)(2,1)S(1)}, bf16[3,128,512]{2,1,0:T(8,128)(2,1)S(1)}, u32[]{:S(2)}, u32[]{:S(2)}) %collective-permute-start.1) | collective-permute-done | bytes 393248 | tf_op jit(solution)/shard_map/ppermute | solution.py:25
  25.7 4.4 %collective-permute-done.2 = bf16[3,128,512]{2,1,0:T(8,128)(2,1)S(1)} collective-permute-done((bf16[3,128,512]{2,1,0:T(8,128)(2,1)S(1)}, bf16[3,128,512]{2,1,0:T(8,128)(2,1)S(1)}, u32[]{:S(2)}, u32[]{:S(2)}) %collective-permute-start.2) | collective-permute-done | bytes 393248 | tf_op jit(solution)/shard_map/ppermute | solution.py:26
  31.4 4.0 %collective-permute-start.3 = (bf16[3,768,128]{2,1,0:T(8,128)(2,1)}, bf16[3,768,128]{2,1,0:T(8,128)(2,1)}, u32[]{:S(2)}, u32[]{:S(2)}) collective-permute-start(bf16[3,768,128]{2,1,0:T(8,128)(2,1)} %get-tuple-element.194), channel_id=1, source_target_pairs={{0,1},{1,2},{2,3},{3,4},{4,5},{5,6},{6,7},{8,9},{9,10},{10,11},{11... | collective-permute-start | bytes 1769480 | tf_op jit(solution)/shard_map/ppermute | solution.py:25
  36.8 4.0 %fusion.71 = bf16[512,512]{1,0:T(8,128)(2,1)S(1)} fusion(), kind=kLoop, calls=%fused_computation.104 | loop fusion | flops 3932160 | bytes 524288 | tf_op jit(solution)/shard_map/convert.13
  40.7 4.3 %negate_convert_fusion.2 = (bf16[512,512]{1,0:T(8,128)(2,1)S(1)}, bf16[512,512]{1,0:T(8,128)(2,1)S(1)}) fusion(), kind=kLoop, calls=%fused_computation.95 | loop fusion | flops 4456448 | bytes 1048576 | tf_op jit(solution)/shard_map/convert.15
  46.3 11.3 %collective-permute-done.4 = bf16[3,768,128]{2,1,0:T(8,128)(2,1)} collective-permute-done((bf16[3,768,128]{2,1,0:T(8,128)(2,1)}, bf16[3,768,128]{2,1,0:T(8,128)(2,1)}, u32[]{:S(2)}, u32[]{:S(2)}) %collective-permute-start.4) | collective-permute-done | bytes 589856 | tf_op jit(solution)/shard_map/ppermute | solution.py:26
  57.6 4.3 %pad_maximum_fusion.7 = bf16[3,768,768]{2,1,0:T(8,128)(2,1)} fusion(bf16[3,768,128]{2,1,0:T(8,128)(2,1)} %collective-permute-done.4, bf16[3,128,512]{2,1,0:T(8,128)(2,1)S(1)} %collective-permute-done.2, bf16[3,512,512]{2,1,0:T(8,128)(2,1)S(1)} %constant_dynamic-update-slice_fusion, bf16[3,128,512]{2,1,0:T(8,128)(2,1)S(1)} %collective-permute-done.1, ...), kind=kLoop, calls=%fused_computation.86 | loop fusion | flops 17694720 | bytes 7077888 | tf_op jit(solution)/shard_map/concatenate | solution.py:27
  62.0 75.7 %while.13 = (s32[]{:T(128)}, f32[4,2,2]{2,1,0:T(2,128)S(1)}, s32[4,2,2]{2,1,0:T(2,128)S(1)}, s32[4]{0:T(128)S(1)}, bf16[3,768,768]{2,1,0:T(8,128)(2,1)}, /*index...) while((s32[]{:T(128)}, f32[4,2,2]{2,1,0:T(2,128)S(1)}, ...), condition=%wide.region_4.5_spmd, body=%wide.region_0.4_spmd.sunk | while | flops 5477073920 | bytes 42212972 | solution.py:173
  65.1 3.5 %convolution_convert_fusion.2 = bf16[3,512,1024]{2,1,0:T(8,128)(2,1)S(1)} fusion(bf16[3,768,768]{2,1,0:T(8,128)(2,1)} %get-tuple-element.311, s32[]{:T(128)S(6)} %select_n.116, s32[]{:T(128)S(6)} %select_n.118, bf16[512,1024]{1,0:T(8,128)(2,1)} %get-tuple-element.312), kind=kOutput, calls=%fused_computation.14.clone.1 | convolution fusion | flops 1612185600 | bytes 5767176 | tf_op jit(solution)/shard_map/while/body/eval_jaxpr/nxy,yk->nxk/dot_general | solution.py:86
  70.8 1.9 %fusion.103 = bf16[3,512,512]{1,2,0:T(8,128)(2,1)S(1)} fusion(bf16[3,512,512]{2,1,0:T(8,128)(2,1)S(1)} %get-tuple-element.263, bf16[3,512,512]{2,1,0:T(8,128)(2,1)S(1)} %get-tuple-element.264, bf16[512,1024]{1,0:T(8,128)(2,1)S(1)} %copy-done), kind=kOutput, calls=%fused_computation.22.clone.1 | convolution fusion | flops 1618477056 | bytes 5767168 | tf_op jit(solution)/shard_map/while/body/eval_jaxpr/kx,nxm->nkm/dot_general | solution.py:98
  73.6 2.5 %negate_convert_fusion.4 = (bf16[2,128,512]{2,1,0:T(8,128)(2,1)S(1)}, bf16[2,128,512]{2,1,0:T(8,128)(2,1)S(1)}, bf16[2,128,512]{2,1,0:T(8,128)(2,1)S(1)}) fusion(s32[2,128]{1,0:T(2,128)S(1)} %get-tuple-element.269), kind=kLoop, calls=%fused_computation.56.clone.1 | loop fusion | flops 2359296 | bytes 787456 | tf_op jit(solution)/shard_map/convert.3
  77.9 2.5 %cosine_convert_fusion.4 = (bf16[2,128,512]{2,1,0:T(8,128)(2,1)S(1)}, bf16[2,128,512]{2,1,0:T(8,128)(2,1)S(1)}) fusion(s32[2,128]{1,0:T(2,128)S(1)} %get-tuple-element.273), kind=kLoop, calls=%fused_computation.61.clone.1 | loop fusion | flops 2228224 | bytes 525312 | tf_op jit(solution)/shard_map/convert.10
  84.0 3.5 %convolution_convert_fusion.2 = bf16[3,512,1024]{2,1,0:T(8,128)(2,1)S(1)} fusion(bf16[3,768,768]{2,1,0:T(8,128)(2,1)} %get-tuple-element.311, s32[]{:T(128)S(6)} %select_n.116, s32[]{:T(128)S(6)} %select_n.118, bf16[512,1024]{1,0:T(8,128)(2,1)} %get-tuple-element.312), kind=kOutput, calls=%fused_computation.14.clone.1 | convolution fusion | flops 1612185600 | bytes 5767176 | tf_op jit(solution)/shard_map/while/body/eval_jaxpr/nxy,yk->nxk/dot_general | solution.py:86
  92.5 2.5 %negate_convert_fusion.4 = (bf16[2,128,512]{2,1,0:T(8,128)(2,1)S(1)}, bf16[2,128,512]{2,1,0:T(8,128)(2,1)S(1)}, bf16[2,128,512]{2,1,0:T(8,128)(2,1)S(1)}) fusion(s32[2,128]{1,0:T(2,128)S(1)} %get-tuple-element.269), kind=kLoop, calls=%fused_computation.56.clone.1 | loop fusion | flops 2359296 | bytes 787456 | tf_op jit(solution)/shard_map/convert.3
  96.9 2.5 %cosine_convert_fusion.4 = (bf16[2,128,512]{2,1,0:T(8,128)(2,1)S(1)}, bf16[2,128,512]{2,1,0:T(8,128)(2,1)S(1)}) fusion(s32[2,128]{1,0:T(2,128)S(1)} %get-tuple-element.273), kind=kLoop, calls=%fused_computation.61.clone.1 | loop fusion | flops 2228224 | bytes 525312 | tf_op jit(solution)/shard_map/convert.10
  102.9 3.5 %convolution_convert_fusion.2 = bf16[3,512,1024]{2,1,0:T(8,128)(2,1)S(1)} fusion(bf16[3,768,768]{2,1,0:T(8,128)(2,1)} %get-tuple-element.311, s32[]{:T(128)S(6)} %select_n.116, s32[]{:T(128)S(6)} %select_n.118, bf16[512,1024]{1,0:T(8,128)(2,1)} %get-tuple-element.312), kind=kOutput, calls=%fused_computation.14.clone.1 | convolution fusion | flops 1612185600 | bytes 5767176 | tf_op jit(solution)/shard_map/while/body/eval_jaxpr/nxy,yk->nxk/dot_general | solution.py:86
  108.7 1.9 %fusion.103 = bf16[3,512,512]{1,2,0:T(8,128)(2,1)S(1)} fusion(bf16[3,512,512]{2,1,0:T(8,128)(2,1)S(1)} %get-tuple-element.263, bf16[3,512,512]{2,1,0:T(8,128)(2,1)S(1)} %get-tuple-element.264, bf16[512,1024]{1,0:T(8,128)(2,1)S(1)} %copy-done), kind=kOutput, calls=%fused_computation.22.clone.1 | convolution fusion | flops 1618477056 | bytes 5767168 | tf_op jit(solution)/shard_map/while/body/eval_jaxpr/kx,nxm->nkm/dot_general | solution.py:98
  111.4 2.5 %negate_convert_fusion.4 = (bf16[2,128,512]{2,1,0:T(8,128)(2,1)S(1)}, bf16[2,128,512]{2,1,0:T(8,128)(2,1)S(1)}, bf16[2,128,512]{2,1,0:T(8,128)(2,1)S(1)}) fusion(s32[2,128]{1,0:T(2,128)S(1)} %get-tuple-element.269), kind=kLoop, calls=%fused_computation.56.clone.1 | loop fusion | flops 2359296 | bytes 787456 | tf_op jit(solution)/shard_map/convert.3
  115.8 2.5 %cosine_convert_fusion.4 = (bf16[2,128,512]{2,1,0:T(8,128)(2,1)S(1)}, bf16[2,128,512]{2,1,0:T(8,128)(2,1)S(1)}) fusion(s32[2,128]{1,0:T(2,128)S(1)} %get-tuple-element.273), kind=kLoop, calls=%fused_computation.61.clone.1 | loop fusion | flops 2228224 | bytes 525312 | tf_op jit(solution)/shard_map/convert.10
  121.9 3.5 %convolution_convert_fusion.2 = bf16[3,512,1024]{2,1,0:T(8,128)(2,1)S(1)} fusion(bf16[3,768,768]{2,1,0:T(8,128)(2,1)} %get-tuple-element.311, s32[]{:T(128)S(6)} %select_n.116, s32[]{:T(128)S(6)} %select_n.118, bf16[512,1024]{1,0:T(8,128)(2,1)} %get-tuple-element.312), kind=kOutput, calls=%fused_computation.14.clone.1 | convolution fusion | flops 1612185600 | bytes 5767176 | tf_op jit(solution)/shard_map/while/body/eval_jaxpr/nxy,yk->nxk/dot_general | solution.py:86
  127.6 1.9 %fusion.103 = bf16[3,512,512]{1,2,0:T(8,128)(2,1)S(1)} fusion(bf16[3,512,512]{2,1,0:T(8,128)(2,1)S(1)} %get-tuple-element.263, bf16[3,512,512]{2,1,0:T(8,128)(2,1)S(1)} %get-tuple-element.264, bf16[512,1024]{1,0:T(8,128)(2,1)S(1)} %copy-done), kind=kOutput, calls=%fused_computation.22.clone.1 | convolution fusion | flops 1618477056 | bytes 5767168 | tf_op jit(solution)/shard_map/while/body/eval_jaxpr/kx,nxm->nkm/dot_general | solution.py:98
  130.4 2.5 %negate_convert_fusion.4 = (bf16[2,128,512]{2,1,0:T(8,128)(2,1)S(1)}, bf16[2,128,512]{2,1,0:T(8,128)(2,1)S(1)}, bf16[2,128,512]{2,1,0:T(8,128)(2,1)S(1)}) fusion(s32[2,128]{1,0:T(2,128)S(1)} %get-tuple-element.269), kind=kLoop, calls=%fused_computation.56.clone.1 | loop fusion | flops 2359296 | bytes 787456 | tf_op jit(solution)/shard_map/convert.3
  134.7 2.5 %cosine_convert_fusion.4 = (bf16[2,128,512]{2,1,0:T(8,128)(2,1)S(1)}, bf16[2,128,512]{2,1,0:T(8,128)(2,1)S(1)}) fusion(s32[2,128]{1,0:T(2,128)S(1)} %get-tuple-element.273), kind=kLoop, calls=%fused_computation.61.clone.1 | loop fusion | flops 2228224 | bytes 525312 | tf_op jit(solution)/shard_map/convert.10
  137.9 4.6 %all_gather.27 = f32[2,1,16]{2,1,0:T(1,128)S(1)} all-gather(f32[1,1,16]{2,1,0:T(1,128)S(1)} %all_gather_reshape.3), channel_id=1, replica_groups=mesh['gz'=2,'row_0'=4,'row_1'=2,'col_0'=4,'col_1'=2] {'gz'}, dimensions={0}, use_global_device_ids=true | all-gather | bytes 192 | tf_op jit(solution)/shard_map/all_gather | solution.py:47
  142.5 3.1 %all-gather = f32[4,1,16]{2,1,0:T(1,128)S(1)} all-gather(f32[2,1,16]{2,1,0:T(1,128)S(1)} %all_gather.27), channel_id=2, replica_groups=mesh['gz'=2,'row_0'=4,'row_1'=2,'col_0'=4,'col_1'=2] {'col_1'}, dimensions={0}, use_global_device_ids=true | all-gather | bytes 384 | tf_op jit(solution)/shard_map/all_gather | solution.py:47
  145.6 9.0 %all-gather.1 = f32[8,2,1,16]{3,1,2,0:T(2,128)S(1)} all-gather(f32[2,2,1,16]{3,1,2,0:T(2,128)S(1)} %bitcast.81), channel_id=3, replica_groups=mesh['gz'=2,'row_0'=4,'row_1'=2,'col_0'=4,'col_1'=2] {'col_0'}, dimensions={0}, use_global_device_ids=true | all-gather | bytes 1280 | tf_op jit(solution)/shard_map/all_gather | solution.py:47
  154.6 2.1 %all-gather.2 = f32[8,2,2,1,16]{4,2,3,1,0:T(2,128)S(1)} all-gather(f32[4,2,2,1,16]{4,2,3,1,0:T(2,128)S(1)} %bitcast.78), channel_id=4, replica_groups=mesh['gz'=2,'row_0'=4,'row_1'=2,'col_0'=4,'col_1'=2] {'row_1'}, dimensions={0}, use_global_device_ids=true | all-gather | bytes 3072 | tf_op jit(solution)/shard_map/all_gather | solution.py:47
  156.8 18.0 %all-gather.3 = f32[8,4,2,2,1,16]{5,1,4,3,2,0:T(4,128)S(1)} all-gather(f32[2,4,2,2,1,16]{5,1,4,3,2,0:T(4,128)S(1)} %copy.34), channel_id=5, replica_groups=mesh['gz'=2,'row_0'=4,'row_1'=2,'col_0'=4,'col_1'=2] {'row_0'}, dimensions={0}, use_global_device_ids=true | all-gather | bytes 10240 | tf_op jit(solution)/shard_map/all_gather | solution.py:47
  (87 shorter events, 34.2 us)
Async XLA Ops:
  1.1 14.9 %collective-permute-start = (bf16[1,512,512]{2,1,0:T(8,128)(2,1)S(1)}, bf16[1,512,512]{2,1,0:T(8,128)(2,1)S(1)}, u32[]{:S(2)}, u32[]{:S(2)}) collective-permute-start(bf16[1,512,512]{2,1,0:T(8,128)(2,1)S(1)} %slice.97), channel_id=1, source_target_pairs={{0,64},{64,0},{1,65},{65,1},{2,66},{66,2},{3,67},{67,3},{4,68},{68... | collective-permute-start | bytes 1572872 | tf_op jit(solution)/shard_map/ppermute | solution.py:34
  16.1 20.6 %copy-start.1 = (s32[2,2,2,2]{3,2,1,0:T(2,128)S(1)}, s32[2,2,2,2]{3,2,1,0:T(2,128)}, u32[]{:S(2)}) copy-start(s32[2,2,2,2]{3,2,1,0:T(2,128)} %param.6) | copy-start | bytes 196
  16.1 9.7 %collective-permute-start.1 = (bf16[3,128,512]{2,1,0:T(8,128)(2,1)S(1)}, bf16[3,128,512]{2,1,0:T(8,128)(2,1)S(1)}, u32[]{:S(2)}, u32[]{:S(2)}) collective-permute-start(bf16[3,128,512]{2,1,0:T(8,128)(2,1)S(1)} %get-tuple-element.196), channel_id=1, source_target_pairs={{0,8},{8,16},{16,24},{24,32},{32,40},{40,48},{48,56},{1,9},{9,17},... | collective-permute-start | bytes 1179656 | tf_op jit(solution)/shard_map/ppermute | solution.py:25
  21.0 9.1 %collective-permute-start.2 = (bf16[3,128,512]{2,1,0:T(8,128)(2,1)S(1)}, bf16[3,128,512]{2,1,0:T(8,128)(2,1)S(1)}, u32[]{:S(2)}, u32[]{:S(2)}) collective-permute-start(bf16[3,128,512]{2,1,0:T(8,128)(2,1)S(1)} %get-tuple-element.197), channel_id=1, source_target_pairs={{8,0},{16,8},{24,16},{32,24},{40,32},{48,40},{56,48},{9,1},{17,9},... | collective-permute-start | bytes 1179656 | tf_op jit(solution)/shard_map/ppermute | solution.py:26
  31.4 15.0 %collective-permute-start.3 = (bf16[3,768,128]{2,1,0:T(8,128)(2,1)}, bf16[3,768,128]{2,1,0:T(8,128)(2,1)}, u32[]{:S(2)}, u32[]{:S(2)}) collective-permute-start(bf16[3,768,128]{2,1,0:T(8,128)(2,1)} %get-tuple-element.194), channel_id=1, source_target_pairs={{0,1},{1,2},{2,3},{3,4},{4,5},{5,6},{6,7},{8,9},{9,10},{10,11},{11... | collective-permute-start | bytes 1769480 | tf_op jit(solution)/shard_map/ppermute | solution.py:25
  35.3 22.3 %collective-permute-start.4 = (bf16[3,768,128]{2,1,0:T(8,128)(2,1)}, bf16[3,768,128]{2,1,0:T(8,128)(2,1)}, u32[]{:S(2)}, u32[]{:S(2)}) collective-permute-start(bf16[3,768,128]{2,1,0:T(8,128)(2,1)} %get-tuple-element.195), channel_id=1, source_target_pairs={{1,0},{2,1},{3,2},{4,3},{5,4},{6,5},{7,6},{9,8},{10,9},{11,10},{12... | collective-permute-start | bytes 1769480 | tf_op jit(solution)/shard_map/ppermute | solution.py:26
  62.0 75.9 %copy-start.2 = (s32[16]{0:T(128)S(1)}, s32[16]{0:T(128)}, u32[]{:S(2)}) copy-start(s32[16]{0:T(128)} %param.7) | copy-start | bytes 196
  68.9 1.9 %copy-start = (bf16[512,1024]{1,0:T(8,128)(2,1)S(1)}, bf16[512,1024]{1,0:T(8,128)(2,1)}, u32[]{:S(2)}) copy-start(bf16[512,1024]{1,0:T(8,128)(2,1)} %get-tuple-element.312) | copy-start | bytes 3145732 | tf_op jit(solution)/shard_map/while
  87.8 1.9 %copy-start = (bf16[512,1024]{1,0:T(8,128)(2,1)S(1)}, bf16[512,1024]{1,0:T(8,128)(2,1)}, u32[]{:S(2)}) copy-start(bf16[512,1024]{1,0:T(8,128)(2,1)} %get-tuple-element.312) | copy-start | bytes 3145732 | tf_op jit(solution)/shard_map/while
  106.8 1.9 %copy-start = (bf16[512,1024]{1,0:T(8,128)(2,1)S(1)}, bf16[512,1024]{1,0:T(8,128)(2,1)}, u32[]{:S(2)}) copy-start(bf16[512,1024]{1,0:T(8,128)(2,1)} %get-tuple-element.312) | copy-start | bytes 3145732 | tf_op jit(solution)/shard_map/while
  125.7 1.9 %copy-start = (bf16[512,1024]{1,0:T(8,128)(2,1)S(1)}, bf16[512,1024]{1,0:T(8,128)(2,1)}, u32[]{:S(2)}) copy-start(bf16[512,1024]{1,0:T(8,128)(2,1)} %get-tuple-element.312) | copy-start | bytes 3145732 | tf_op jit(solution)/shard_map/while
where the time goes:
time: 179 us; the launch traced here: 177 us
  matrix products  39 us (22%)
  other arithmetic  38.4 us (21%)
  blocking collectives  36.8 us (21%)
  waiting for transfers between devices  28.4 us (16%)
  starting transfers between devices  15.8 us (9%)
  loops' own time  10.6 us (6%)
  local copies, waits for them, and re-layouts  7.66 us (4%)
    all_gather x5, blocking collectives, all_blocks(): parts = lax.all_gather(parts, axes[k])  36.8 us
    another operation x11, other arithmetic  28 us
    ppermute x2, waiting for transfers between devices, with_halo(): after = lax.ppermute(first, axis, down)  15.7 us
    dot_general x4, matrix products, spectra_of(): jnp.einsum('nxy,yk->nxk', patches, minus_table, preferred_element_type=jn...  14.1 us
    another operation x1, loops' own time, body(): all_flows = lax.map(place_flows, (positions, offsets_all))  10.6 us
    ppermute x1, waiting for transfers between devices, shifted(): return lax.ppermute(value, axis, pairs)  9.94 us
    ppermute x2, starting transfers between devices, with_halo(): before = lax.ppermute(last, axis, up)  8.93 us
    dot_general x4, matrix products, spectra_of(): jnp.einsum('kx,nxm->nkm', minus_table, lower_stack, preferred_element_typ...  7.52 us
  transfers between devices with their start and end apart: 5, of which 4 were waited for; matrix products, arithmetic and copies ran while one was open for 6% of the time, Pallas kernels for 0%

commit v1 on v0

v1 whole, which is shorter than its diff:
```python
import functools

import jax
import jax.numpy as jnp
import ml_dtypes
import numpy as np
from jax import lax
from jax.experimental import pallas as pl
from jax.experimental.pallas import tpu as pltpu
from jax.sharding import PartitionSpec as P

PATCH = 512
LAGS = 128
UNIT = 128
MESH = pl.DeviceIdType.MESH
BF16 = jnp.bfloat16
F32 = jnp.float32


def slots():
    m = np.arange(128)
    freq = np.concatenate([2 * m, 2 * m, 2 * m + 1, 2 * m + 1])
    sine = np.concatenate([np.zeros(128), np.ones(128), np.zeros(128), np.ones(128)]).astype(bool)
    weight = np.full(512, 2.0)
    freq[128], sine[128] = 256, False
    weight[0] = weight[128] = 1.0
    return freq, sine, weight


def forward_table():
    freq, sine, _ = slots()
    angle = (freq[:, None] * np.arange(PATCH)[None, :]) % PATCH * (2.0 * np.pi / PATCH)
    return np.where(sine[:, None], np.sin(angle), np.cos(angle)).astype(ml_dtypes.bfloat16)


def lag_tables():
    freq, _, weight = slots()
    lag = np.arange(LAGS) - LAGS // 2
    angle = (freq[None, :] * lag[:, None]) % PATCH * (2.0 * np.pi / PATCH)
    return (np.cos(angle) * weight).astype(np.float32), (np.sin(angle) * weight).astype(np.float32)


def phase_rows():
    freq, sine, _ = slots()
    rows = np.zeros((8, 512), np.int32)
    rows[0] = freq
    rows[1] = np.where(sine, -128, 0)
    rows[2] = np.where(sine, 0, 128)
    rows[3] = 1
    rows[3, 128] = 0
    return rows


def cross_chunk(a, b, m_ref, kb, lb, rc):
    top = pl.multiple_of(kb * 256 + rc * 16, 16)
    low = pl.multiple_of(kb * 256 + 128 + rc * 16, 16)
    lc, ls = pl.ds(lb * 256, 128), pl.ds(lb * 256 + 128, 128)
    rt, rl = pl.ds(top, 16), pl.ds(low, 16)
    a1, a2, a3, a4 = a[rt, lc], a[rt, ls], a[rl, lc], a[rl, ls]
    b1, b2, b3, b4 = b[rt, lc], b[rt, ls], b[rl, lc], b[rl, ls]
    p33, p44 = a3 * b3, a4 * b4
    u1, u2 = a1 * b2 - a2 * b1, a3 * b4 - a4 * b3
    v1, v2 = a1 * b3 - a3 * b1, a2 * b4 - a4 * b2
    ss = (a1 * b4 + a4 * b1) - (a2 * b3 + a3 * b2)
    if kb == 0:
        k0 = lax.broadcasted_iota(jnp.int32, (16, 128), 0) + rc * 16 == 0
        z33, z44, zu2 = jnp.where(k0, 0.0, p33), jnp.where(k0, 0.0, p44), jnp.where(k0, 0.0, u2)
    else:
        z33, z44, zu2 = p33, p44, u2
    t1, t2 = a1 * b1 + z33, a2 * b2 + z44
    cc, cs, sc = t1 + t2, u1 + zu2, v1 + v2
    if kb == 0:
        sc, ss = jnp.where(k0, p33 + p44, sc), jnp.where(k0, u2, ss)
    if lb == 0:
        l0 = lax.broadcasted_iota(jnp.int32, (16, 128), 1) == 0
        cc, cs = jnp.where(l0, t1, cc), jnp.where(l0, t2, cs)
        if kb == 0:
            sc = jnp.where(l0, jnp.where(k0, p33, v1), sc)
            ss = jnp.where(l0, jnp.where(k0, p44, v2), ss)
        else:
            sc, ss = jnp.where(l0, v1, sc), jnp.where(l0, v2, ss)
    m_ref[rt, lc] = cc.astype(BF16)
    m_ref[rt, ls] = cs.astype(BF16)
    m_ref[rl, lc] = sc.astype(BF16)
    m_ref[rl, ls] = ss.astype(BF16)


def kernel(
    sections, priors, row_order, table, table_t, lag_cos, lag_sin, phases, out,
    m_buf, pg_buf, zm, zpg, a_s, b_s, mix, prior_own, prior_guest, u_s, v_s, sums, flow_send, flow_recv, grid_send, grid_recv,
    local_sem, send_x, recv_x, send_r, recv_r, send_p, recv_p, send_c, recv_c,
):
    gz, row, col = lax.axis_index("gz"), lax.axis_index("row"), lax.axis_index("col")
    n_gz, n_row, n_col = lax.axis_size("gz"), lax.axis_size("row"), lax.axis_size("col")
    x_lo = lax.rem(col, 2)
    z = lax.div(col, 2)
    has_left, has_right = z > 0, z < n_col // 2 - 1
    has_out = jnp.logical_or(jnp.logical_and(x_lo == 0, has_left), jnp.logical_and(x_lo == 1, has_right))
    has_in = jnp.logical_or(jnp.logical_and(x_lo == 1, has_left), jnp.logical_and(x_lo == 0, has_right))
    has_up, has_down = row > 0, row < n_row - 1
    side = 2 * x_lo - 1
    a_id = (gz, row, col - side)
    b_id = (1 - gz, row, col - side)
    n_id = (gz, row, col + side)
    z_out = (gz, row, col + 2 * side)
    z_in = (gz, row, col - 2 * side)
    up_id, down_id = (gz, row - 1, col), (gz, row + 1, col)

    def al(v):
        return pl.multiple_of(v, 128)

    c0 = al(128 + 512 * x_lo)
    near, outer = al(512 + 128 * x_lo), al(128 + 896 * x_lo)
    near_p, outer_p = al(512 - 384 * x_lo), al(128 + 384 * x_lo)
    c1 = al(640 - 512 * x_lo)
    near_g, outer_g = al(640 - 128 * x_lo), al(1024 - 896 * x_lo)
    m_far_out, m_far_in = al(1152 * x_lo), al(1152 - 1152 * x_lo)
    side_in, side_out = al(640 - 640 * x_lo), al(640 * x_lo)
    body = pl.ds(128, 512)
    p_buf, g_buf = pg_buf.at[0], pg_buf.at[1]

    own_m = pltpu.make_async_copy(sections.at[x_lo], m_buf.at[body, pl.ds(c0, 512)], local_sem.at[0])
    own_p = pltpu.make_async_copy(sections.at[1 - x_lo], p_buf.at[body, pl.ds(128, 512)], local_sem.at[1])
    own_m.start()
    own_p.start()

    peers_plane = [(lax.rem(gz + dg, n_gz), row, lax.rem(col + dc, n_col)) for dg in range(n_gz) for dc in range(n_col) if dg or dc]
    peers_column = [(gz, lax.rem(row + d, n_row), col) for d in range(1, n_row)]
    barrier = pltpu.get_barrier_semaphore()
    for peer in peers_plane + peers_column:
        pl.semaphore_signal(barrier, inc=1, device_id=peer, device_id_type=MESH)

    for c in range(2):
        for ii in range(2):
            for jj in range(2):
                r = c * 4 + ii * 2 + jj
                prior_own[0, r : r + 1, :] = jnp.full((1, 128), priors[c, 0, ii, jj], jnp.int32)
                prior_own[1, r : r + 1, :] = jnp.full((1, 128), priors[c, 1, ii, jj], jnp.int32)

    @pl.when(row == 0)
    def _():
        m_buf[0:128, :] = jnp.zeros((128, 1280), BF16)
        pg_buf[:, 0:128, :] = jnp.zeros((2, 128, 768), BF16)

    @pl.when(row == n_row - 1)
    def _():
        m_buf[640:768, :] = jnp.zeros((128, 1280), BF16)
        pg_buf[:, 640:768, :] = jnp.zeros((2, 128, 768), BF16)

    @pl.when(jnp.logical_not(has_left))
    def _():
        m_buf[:, 0:128] = jnp.zeros((768, 128), BF16)
        pg_buf[x_lo, :, 0:128] = jnp.zeros((768, 128), BF16)

    @pl.when(jnp.logical_not(has_right))
    def _():
        m_buf[:, 1152:1280] = jnp.zeros((768, 128), BF16)
        pg_buf[1 - x_lo, :, 640:768] = jnp.zeros((768, 128), BF16)

    own_m.wait()
    own_p.wait()
    pl.semaphore_wait(barrier, len(peers_plane) + len(peers_column))

    def remote(k, src, dst, device):
        return pltpu.make_async_remote_copy(
            src_ref=src, dst_ref=dst, send_sem=send_x.at[k], recv_sem=recv_x.at[k], device_id=device, device_id_type=MESH
        )

    def strip(ref, start, width=128):
        return ref.at[body, pl.ds(start, width)]

    pa_outer = remote(0, strip(p_buf, outer_p), strip(m_buf, outer), a_id)
    pa_near = remote(1, strip(p_buf, near_p), strip(m_buf, near), a_id)
    m_a = remote(2, strip(m_buf, near), strip(p_buf, side_out), a_id)
    m_n = remote(3, strip(m_buf, outer), strip(p_buf, side_in), n_id)
    pa_mid = remote(4, strip(p_buf, 256, 256), strip(m_buf, al(c0 + 128), 256), a_id)
    mz_own = remote(5, strip(m_buf, outer), strip(m_buf, m_far_in), z_out)
    mb_tile = remote(6, strip(m_buf, c0, 512), strip(g_buf, 128, 512), b_id)
    mz_guest = remote(7, strip(m_buf, outer_g), strip(m_buf, m_far_out), z_in)
    mb_near = remote(8, strip(m_buf, near_g), strip(g_buf, side_in), b_id)
    mb_far = remote(9, strip(m_buf, m_far_out), strip(g_buf, side_out), b_id)
    prior_id = (gz + x_lo * (1 - 2 * gz), row, col - side)
    prior_send = remote(10, prior_own.at[1], prior_guest, prior_id)

    prior_send.start()
    pa_outer.start()
    mb_tile.start()
    pl.when(has_out)(mz_own.start)
    pa_near.start()
    m_a.start()
    pl.when(has_out)(m_n.start)
    pa_mid.start()

    landed = {
        0: strip(m_buf, outer_g), 1: strip(m_buf, near_g), 2: strip(p_buf, side_in), 3: strip(p_buf, side_out),
        4: strip(m_buf, al(c1 + 128), 256), 5: strip(m_buf, m_far_in), 6: strip(g_buf, 128, 512), 7: strip(m_buf, m_far_out),
        8: strip(g_buf, side_out), 9: strip(g_buf, side_in), 10: prior_guest,
    }
    when_recv = {3: has_out, 5: has_in, 7: has_out, 9: has_in}

    def landing(k):
        ref = landed[k]
        return remote(k, ref, ref, a_id)

    def rows_of(k, ref, start, width):
        cols = pl.ds(start, width)
        up = pltpu.make_async_remote_copy(
            src_ref=ref.at[pl.ds(128, 128), cols], dst_ref=ref.at[pl.ds(640, 128), cols],
            send_sem=send_r.at[2 * k], recv_sem=recv_r.at[2 * k], device_id=up_id, device_id_type=MESH,
        )
        down = pltpu.make_async_remote_copy(
            src_ref=ref.at[pl.ds(512, 128), cols], dst_ref=ref.at[pl.ds(0, 128), cols],
            send_sem=send_r.at[2 * k + 1], recv_sem=recv_r.at[2 * k + 1], device_id=down_id, device_id_type=MESH,
        )
        return up, down

    pieces = {
        0: (m_buf, outer_g, 128), 1: (m_buf, near_g, 128), 2: (p_buf, side_in, 128), 3: (p_buf, side_out, 128),
        4: (m_buf, al(c1 + 128), 256), 5: (m_buf, m_far_in, 128), 6: (g_buf, 128, 512), 7: (m_buf, m_far_out, 128),
        8: (g_buf, side_out, 128), 9: (g_buf, side_in, 128), 10: (m_buf, c0, 512), 11: (p_buf, 128, 512),
    }

    def send_rows(k):
        up, down = rows_of(k, *pieces[k])
        pl.when(has_up)(up.start)
        pl.when(has_down)(down.start)

    def wait_rows(k):
        up, down = rows_of(k, *pieces[k])
        pl.when(has_down)(up.wait_recv)
        pl.when(has_up)(down.wait_recv)

    def wait_sent_rows(k):
        up, down = rows_of(k, *pieces[k])
        pl.when(has_up)(up.wait_send)
        pl.when(has_down)(down.wait_send)

    def guarded(k, do):
        if k in when_recv:
            pl.when(when_recv[k])(do)
        else:
            do()

    def arrive(k, forward=None, cond=None):
        def do():
            landing(k).wait_recv()
            send_rows(k)

        guarded(k, do)
        if forward is not None:
            if cond is None:
                forward.start()
            else:
                pl.when(cond)(forward.start)

    send_rows(10)
    send_rows(11)
    landing(10).wait_recv()

    freq, off_u, off_v, mask_v = phases[0:1, :], phases[1:2, :], phases[2:3, :], phases[3:4, :]
    for t in range(2):
        value = prior_own[0] if t == 0 else prior_guest[...]
        sign = (1 - 2 * x_lo) * (1 - 2 * t)
        wide = jnp.concatenate([value] * 4, axis=1) * sign
        turn = wide * freq
        scale = 2.0 * np.pi / PATCH
        u_s[8 * t : 8 * t + 8, :] = jnp.cos(((turn + off_u) & (PATCH - 1)).astype(F32) * scale)
        v_s[8 * t : 8 * t + 8, :] = (
            jnp.cos(((turn + off_v) & (PATCH - 1)).astype(F32) * scale) * mask_v.astype(F32) * sign.astype(F32)
        )

    arrive(0, mz_guest, has_in)
    arrive(5)
    arrive(1, mb_near)
    arrive(2)
    arrive(3)
    arrive(7, mb_far, has_out)
    arrive(4)
    arrive(6)
    arrive(8)
    arrive(9)
    for k in range(12):
        guarded(k, functools.partial(wait_rows, k))

    def first_pass(src, dst, block):
        at = al(block * 256)
        for i in range(2):
            dst[i, :, pl.ds(at, 256)] = jnp.dot(
                table[...], src[pl.ds(256 * i, 512), pl.ds(at, 256)], preferred_element_type=F32
            ).astype(BF16)

    pl.loop(0, 5)(lambda b: first_pass(m_buf, zm, b))
    pl.loop(0, 3)(lambda b: first_pass(p_buf, zpg.at[0], b))
    pl.loop(0, 3)(lambda b: first_pass(g_buf, zpg.at[1], b))

    reach = (lax.broadcasted_iota(jnp.int32, (LAGS, LAGS), 0) - LAGS // 2).astype(F32)
    unit = 1.0 / (512.0 * 512.0 * 512.0)

    def lag_table(r):
        return (lag_cos[...] * u_s[pl.ds(r, 1), :] + lag_sin[...] * v_s[pl.ds(r, 1), :]).astype(BF16)

    @pl.loop(0, 8)
    def _(n):
        t = n // 4
        i = (n // 2) % 2
        j = n % 2
        tile = x_lo + t * (1 - 2 * x_lo)
        at_m = al((tile * 2 + j) * 256)
        at_x = al(j * 256)
        a_s[...] = jnp.dot(zm[i, :, pl.ds(at_m, 512)], table_t[...], preferred_element_type=F32)
        b_s[...] = jnp.dot(zpg[t, i, :, pl.ds(at_x, 512)], table_t[...], preferred_element_type=F32)

        @pl.loop(0, 8)
        def _(rc):
            for kb in range(2):
                for lb in range(2):
                    cross_chunk(a_s, b_s, mix, kb, lb, rc)

        rows = lag_table(8 * t + i * 2 + j)
        columns = lag_table(8 * t + 4 + i * 2 + j)
        half = jnp.dot(rows, mix[...], preferred_element_type=F32).astype(BF16)
        surface = lax.dot_general(half, columns, (((1,), (1,)), ((), ())), preferred_element_type=F32) * unit
        weights = surface * surface
        sums[0, pl.ds(n, 1), :] = jnp.sum(weights, axis=0, keepdims=True)
        sums[1, pl.ds(n, 1), :] = jnp.sum(weights * reach, axis=0, keepdims=True)

    lane = lax.broadcasted_iota(jnp.int32, (8, 128), 1)
    along = (lane - LAGS // 2).astype(F32)
    by_pair = sums[0]
    total = 1.0 + jnp.sum(by_pair, axis=1, keepdims=True)
    shift_r = jnp.sum(sums[1], axis=1, keepdims=True) / total
    shift_c = jnp.sum(by_pair * along, axis=1, keepdims=True) / total

    lane1 = lax.broadcasted_iota(jnp.int32, (1, 128), 1)
    guest_s = 3 - 2 * (gz + x_lo - 2 * gz * x_lo)
    for i in range(2):
        line = jnp.zeros((1, 128), F32)
        for t in range(2):
            s = 2 * gz if t == 0 else guest_s
            c_tile = 2 * z + (x_lo if t == 0 else 1 - x_lo)
            held = prior_own[0] if t == 0 else prior_guest[...]
            for j in range(2):
                n = t * 4 + i * 2 + j
                r = i * 2 + j
                place = s * 16 + 2 * c_tile + j
                flow_r = held[r : r + 1, :].astype(F32) + shift_r[n : n + 1, :]
                flow_c = held[4 + r : 5 + r, :].astype(F32) + shift_c[n : n + 1, :]
                line = line + jnp.where(lane1 == place, flow_r, 0.0) + jnp.where(lane1 == place + 64, flow_c, 0.0)
        flow_send[i : i + 1, :] = line

    me_plane = gz * n_col + col

    def to_plane(d, peer):
        return pltpu.make_async_remote_copy(
            src_ref=flow_send, dst_ref=flow_recv.at[me_plane], send_sem=send_p.at[d], recv_sem=recv_p.at[d],
            device_id=peer, device_id_type=MESH,
        )

    offsets = [(dg, dc) for dg in range(n_gz) for dc in range(n_col) if dg or dc]
    for d, peer in enumerate(peers_plane):
        to_plane(d, peer).start()
    lines = flow_send[...]
    for d, (dg, dc) in enumerate(offsets):
        source = lax.rem(gz + n_gz - dg, n_gz) * n_col + lax.rem(col + n_col - dc, n_col)
        pltpu.make_async_remote_copy(
            src_ref=flow_recv.at[source], dst_ref=flow_recv.at[source], send_sem=send_p.at[d], recv_sem=recv_p.at[d],
            device_id=a_id, device_id_type=MESH,
        ).wait_recv()
        lines = lines + flow_recv[source]
    grid_send[...] = lines

    def to_column(d, peer):
        return pltpu.make_async_remote_copy(
            src_ref=grid_send, dst_ref=grid_recv.at[row], send_sem=send_c.at[d], recv_sem=recv_c.at[d],
            device_id=peer, device_id_type=MESH,
        )

    for d, peer in enumerate(peers_column):
        to_column(d, peer).start()
    want = [row_order[2 * row + m] for m in range(2)]
    picked = [jnp.zeros((1, 128), F32) for _ in range(2)]

    def pick(block, owner):
        for m in range(2):
            for i in range(2):
                hit = jnp.full((1, 128), want[m], jnp.int32) == jnp.full((1, 128), 2 * owner + i, jnp.int32)
                picked[m] = picked[m] + jnp.where(hit, block[i : i + 1, :], 0.0)

    pick(lines, row)
    for d in range(n_row - 1):
        source = lax.rem(row + n_row - (d + 1), n_row)
        pltpu.make_async_remote_copy(
            src_ref=grid_recv.at[source], dst_ref=grid_recv.at[source], send_sem=send_c.at[d], recv_sem=recv_c.at[d],
            device_id=a_id, device_id_type=MESH,
        ).wait_recv()
        pick(grid_recv[source], source)
    for m in range(2):
        out[m : m + 1, :] = picked[m]

    sends = [
        (pa_outer, None), (pa_near, None), (m_a, None), (m_n, has_out), (pa_mid, None), (mz_own, has_out), (mb_tile, None),
        (mz_guest, has_in), (mb_near, None), (mb_far, has_out), (prior_send, None),
    ]
    for copy, cond in sends:
        if cond is None:
            copy.wait_send()
        else:
            pl.when(cond)(copy.wait_send)
    for k in range(12):
        guarded(k, functools.partial(wait_sent_rows, k))
    for d, peer in enumerate(peers_plane):
        to_plane(d, peer).wait_send()
    for d, peer in enumerate(peers_column):
        to_column(d, peer).wait_send()


def body(sections, priors, row_order):
    table = forward_table()
    lag_cos, lag_sin = lag_tables()
    vmem = pl.BlockSpec(memory_space=pltpu.VMEM)
    smem = pl.BlockSpec(memory_space=pltpu.SMEM)
    dma = pltpu.SemaphoreType.DMA
    return pl.pallas_call(
        kernel,
        out_shape=jax.ShapeDtypeStruct((2, 128), F32),
        in_specs=[pl.BlockSpec(memory_space=pl.ANY), smem, smem, vmem, vmem, vmem, vmem, vmem],
        out_specs=vmem,
        scratch_shapes=[
            pltpu.VMEM((768, 1280), BF16),
            pltpu.VMEM((2, 768, 768), BF16),
            pltpu.VMEM((2, 512, 1280), BF16),
            pltpu.VMEM((2, 2, 512, 768), BF16),
            pltpu.VMEM((512, 512), F32),
            pltpu.VMEM((512, 512), F32),
            pltpu.VMEM((512, 512), BF16),
            pltpu.VMEM((2, 8, 128), jnp.int32),
            pltpu.VMEM((8, 128), jnp.int32),
            pltpu.VMEM((16, 512), F32),
            pltpu.VMEM((16, 512), F32),
            pltpu.VMEM((2, 8, 128), F32),
            pltpu.VMEM((2, 128), F32),
            pltpu.VMEM((16, 2, 128), F32),
            pltpu.VMEM((2, 128), F32),
            pltpu.VMEM((8, 2, 128), F32),
            dma((2,)),
            dma((11,)),
            dma((11,)),
            dma((24,)),
            dma((24,)),
            dma((15,)),
            dma((15,)),
            dma((7,)),
            dma((7,)),
        ],
        compiler_params=pltpu.CompilerParams(collective_id=0, has_side_effects=True, vmem_limit_bytes=48 * 1024 * 1024),
    )(
        sections, priors, row_order, jnp.asarray(table), jnp.asarray(np.ascontiguousarray(table.T)),
        jnp.asarray(lag_cos), jnp.asarray(lag_sin), jnp.asarray(phase_rows()),
    )


def solution(mesh):
    return jax.shard_map(
        body,
        mesh=mesh,
        in_specs=(P("gz", "row", "col"), P(None, "gz", "row", "col"), P()),
        out_specs=P("row", None),
        check_vma=False,
    )
```

time: 179 us -> 66.3 us (0.37); the launches traced: 177 us -> 65.9 us
  Pallas kernels: 0 us -> 58 us
  matrix products: 39 us -> 0 us
  other arithmetic: 38.4 us -> 0 us
  blocking collectives: 36.8 us -> 0 us
  waiting for transfers between devices: 28.4 us -> 0 us
  starting transfers between devices: 15.8 us -> 0 us
  loops' own time: 10.6 us -> 0 us
    pallas_call x0 -> x1, Pallas kernels: none -> 58 us  [body(): pl.pallas_call(kernel, out_shape=jax.ShapeDtypeStruct((2, 128), F32), in_...]
    dot_general x25 -> x0, matrix products: 39 us -> none  [the longest x4 14.1 us: spectra_of(): jnp.einsum('nxy,yk->nxk', patches, minus_table, preferred_element_type=jn...]
    all_gather x5 -> x0, blocking collectives: 36.8 us -> none  [all_blocks(): parts = lax.all_gather(parts, axes[k])]
    ppermute x5 -> x0, waiting for transfers between devices: 28.4 us -> none  [the longest x2 15.7 us: with_halo(): after = lax.ppermute(first, axis, down)]
    another operation x11 -> x0, other arithmetic: 28 us -> none
    ppermute x5 -> x0, starting transfers between devices: 15.8 us -> none  [the longest x2 8.93 us: with_halo(): before = lax.ppermute(last, axis, up)]
    another operation x1 -> x0, loops' own time: 10.6 us -> none  [body(): all_flows = lax.map(place_flows, (positions, offsets_all))]
    unnamed x5 -> x17, local copies, waits for them, and re-layouts: 1.3 us -> 7.83 us
  transfers between devices with their start and end apart: 5 -> 0, of which waited for: 4 -> 0; matrix products, arithmetic and copies ran while one was open for 6% -> 0% of each run, Pallas kernels for 0% -> 0%
where the time goes in v1:
time: 66.3 us; the launch traced here: 65.9 us
  Pallas kernels  58 us (87%)
  local copies, waits for them, and re-layouts  7.83 us (12%)
    pallas_call x1, Pallas kernels, body(): pl.pallas_call(kernel, out_shape=jax.ShapeDtypeStruct((2, 128), F32), in_...  58 us
    unnamed x17, local copies, waits for them, and re-layouts  7.83 us

profile of v1, /device:TPU:1, one launch (start us, length us, event | category | flops | bytes accessed | tf_op | source)
XLA Modules:
  0.0 65.9 jit_solution(996912448539937128)
XLA Ops:
  0.0 0.0 copy-start
  0.0 1.2 %copy-done = bf16[2,512,512]{2,1,0:T(8,128)(2,1)S(1)} copy-done((bf16[2,512,512]{2,1,0:T(8,128)(2,1)S(1)}, bf16[2,512,512]{2,1,0:T(8,128)(2,1)}, u32[]{:S(2)}) %copy-start) | copy-done | bytes 1048600
  1.2 0.0 copy-start.1
  1.2 1.0 %copy-done.1 = bf16[512,512]{1,0:T(8,128)(2,1)S(1)} copy-done((bf16[512,512]{1,0:T(8,128)(2,1)S(1)}, bf16[512,512]{1,0:T(8,128)(2,1)}, u32[]{:S(2)}) %copy-start.1) | copy-done | bytes 524312
  2.3 0.0 copy-start.2
  2.3 1.0 %copy-done.2 = bf16[512,512]{1,0:T(8,128)(2,1)S(1)} copy-done((bf16[512,512]{1,0:T(8,128)(2,1)S(1)}, bf16[512,512]{1,0:T(8,128)(2,1)}, u32[]{:S(2)}) %copy-start.2) | copy-done | bytes 524312
  3.3 0.0 copy-start.3
  3.3 0.9 %copy-done.3 = f32[128,512]{1,0:T(8,128)S(1)} copy-done((f32[128,512]{1,0:T(8,128)S(1)}, f32[128,512]{1,0:T(8,128)}, u32[]{:S(2)}) %copy-start.3) | copy-done | bytes 262168
  4.3 0.0 copy-start.4
  4.3 0.9 %copy-done.4 = f32[128,512]{1,0:T(8,128)S(1)} copy-done((f32[128,512]{1,0:T(8,128)S(1)}, f32[128,512]{1,0:T(8,128)}, u32[]{:S(2)}) %copy-start.4) | copy-done | bytes 262168
  5.2 0.0 copy-start.5
  5.2 0.7 %copy-done.5 = s32[8,512]{1,0:T(8,128)S(1)} copy-done((s32[8,512]{1,0:T(8,128)S(1)}, s32[8,512]{1,0:T(8,128)}, u32[]{:S(2)}) %copy-start.5) | copy-done | bytes 16408
  5.9 0.0 copy-start.6
  5.9 0.7 %copy-done.6 = s32[2,2,2,2]{3,2,1,0:T(2,128)S(1)} copy-done((s32[2,2,2,2]{3,2,1,0:T(2,128)S(1)}, s32[2,2,2,2]{3,2,1,0:T(2,128)}, u32[]{:S(2)}) %copy-start.6) | copy-done | bytes 88
  6.6 0.0 copy-start.7
  6.6 0.7 copy-done.7
  7.3 58.0 %shard_map.82 = f32[2,128]{1,0:T(2,128)S(1)} custom-call(bf16[2,512,512]{2,1,0:T(8,128)(2,1)S(1)} %copy-done, s32[2,2,2,2]{3,2,1,0:T(2,128)S(1)} %copy-done.6, s32[16]{0:T(128)S(1)} %copy-done.7, bf16[512,512]{1,0:T(8,128)(2,1)S(1)} %copy-done.2, bf16[512,512]{1,0:T(8,128)(2,1)S(1)} %copy-done.1, f32[128,512]{1,0:T(8,128)S(1)} %copy-done.4, ...), custom_call_target="tpu_custom_call" | custom-call | tf_op jit(solution)/shard_map/pallas_call | solution.py:423
  65.3 0.6 copy.10
Async XLA Ops:
  0.0 1.2 %copy-start = (bf16[2,512,512]{2,1,0:T(8,128)(2,1)S(1)}, bf16[2,512,512]{2,1,0:T(8,128)(2,1)}, u32[]{:S(2)}) copy-start(bf16[2,512,512]{2,1,0:T(8,128)(2,1)} %sections.1) | copy-start | bytes 3145732
  1.2 1.0 %copy-start.1 = (bf16[512,512]{1,0:T(8,128)(2,1)S(1)}, bf16[512,512]{1,0:T(8,128)(2,1)}, u32[]{:S(2)}) copy-start(bf16[512,512]{1,0:T(8,128)(2,1)} %constant.11.clone.table_t) | copy-start | bytes 1572868
  2.3 1.0 %copy-start.2 = (bf16[512,512]{1,0:T(8,128)(2,1)S(1)}, bf16[512,512]{1,0:T(8,128)(2,1)}, u32[]{:S(2)}) copy-start(bf16[512,512]{1,0:T(8,128)(2,1)} %constant.10.clone.table) | copy-start | bytes 1572868
  3.3 0.9 %copy-start.3 = (f32[128,512]{1,0:T(8,128)S(1)}, f32[128,512]{1,0:T(8,128)}, u32[]{:S(2)}) copy-start(f32[128,512]{1,0:T(8,128)} %constant.13.clone.lag_sin) | copy-start | bytes 786436
  4.3 0.9 %copy-start.4 = (f32[128,512]{1,0:T(8,128)S(1)}, f32[128,512]{1,0:T(8,128)}, u32[]{:S(2)}) copy-start(f32[128,512]{1,0:T(8,128)} %constant.12.clone.lag_cos) | copy-start | bytes 786436
  5.2 0.7 %copy-start.5 = (s32[8,512]{1,0:T(8,128)S(1)}, s32[8,512]{1,0:T(8,128)}, u32[]{:S(2)}) copy-start(s32[8,512]{1,0:T(8,128)} %constant.14.clone.phases) | copy-start | bytes 49156
  5.9 0.7 %copy-start.6 = (s32[2,2,2,2]{3,2,1,0:T(2,128)S(1)}, s32[2,2,2,2]{3,2,1,0:T(2,128)}, u32[]{:S(2)}) copy-start(s32[2,2,2,2]{3,2,1,0:T(2,128)} %priors.1) | copy-start | bytes 196
  6.6 0.7 copy-start.7

commit v2 on v1

--- a/solution.py
+++ b/solution.py
@@ -52,42 +52,42 @@
 
 
 def cross_chunk(a, b, m_ref, kb, lb, rc):
-    top = pl.multiple_of(kb * 256 + rc * 16, 16)
-    low = pl.multiple_of(kb * 256 + 128 + rc * 16, 16)
     lc, ls = pl.ds(lb * 256, 128), pl.ds(lb * 256 + 128, 128)
-    rt, rl = pl.ds(top, 16), pl.ds(low, 16)
+    rt, rl = pl.ds(rc * 16, 16), pl.ds(128 + rc * 16, 16)
+    mt, ml = pl.ds(kb * 256 + rc * 16, 16), pl.ds(kb * 256 + 128 + rc * 16, 16)
     a1, a2, a3, a4 = a[rt, lc], a[rt, ls], a[rl, lc], a[rl, ls]
     b1, b2, b3, b4 = b[rt, lc], b[rt, ls], b[rl, lc], b[rl, ls]
     p33, p44 = a3 * b3, a4 * b4
     u1, u2 = a1 * b2 - a2 * b1, a3 * b4 - a4 * b3
     v1, v2 = a1 * b3 - a3 * b1, a2 * b4 - a4 * b2
     ss = (a1 * b4 + a4 * b1) - (a2 * b3 + a3 * b2)
-    if kb == 0:
-        k0 = lax.broadcasted_iota(jnp.int32, (16, 128), 0) + rc * 16 == 0
+    first_row = kb == 0 and rc == 0
+    if first_row:
+        k0 = lax.broadcasted_iota(jnp.int32, (16, 128), 0) == 0
         z33, z44, zu2 = jnp.where(k0, 0.0, p33), jnp.where(k0, 0.0, p44), jnp.where(k0, 0.0, u2)
     else:
         z33, z44, zu2 = p33, p44, u2
     t1, t2 = a1 * b1 + z33, a2 * b2 + z44
     cc, cs, sc = t1 + t2, u1 + zu2, v1 + v2
-    if kb == 0:
+    if first_row:
         sc, ss = jnp.where(k0, p33 + p44, sc), jnp.where(k0, u2, ss)
     if lb == 0:
         l0 = lax.broadcasted_iota(jnp.int32, (16, 128), 1) == 0
         cc, cs = jnp.where(l0, t1, cc), jnp.where(l0, t2, cs)
-        if kb == 0:
+        if first_row:
             sc = jnp.where(l0, jnp.where(k0, p33, v1), sc)
             ss = jnp.where(l0, jnp.where(k0, p44, v2), ss)
         else:
             sc, ss = jnp.where(l0, v1, sc), jnp.where(l0, v2, ss)
-    m_ref[rt, lc] = cc.astype(BF16)
-    m_ref[rt, ls] = cs.astype(BF16)
-    m_ref[rl, lc] = sc.astype(BF16)
-    m_ref[rl, ls] = ss.astype(BF16)
+    m_ref[mt, lc] = cc.astype(BF16)
+    m_ref[mt, ls] = cs.astype(BF16)
+    m_ref[ml, lc] = sc.astype(BF16)
+    m_ref[ml, ls] = ss.astype(BF16)
 
 
 def kernel(
-    sections, priors, row_order, table, table_t, lag_cos, lag_sin, phases, out,
-    m_buf, pg_buf, zm, zpg, a_s, b_s, mix, prior_own, prior_guest, u_s, v_s, sums, flow_send, flow_recv, grid_send, grid_recv,
+    sections, priors_h, row_order_h, table_h, table_t_h, lag_cos_h, lag_sin_h, phases_h, out,
+    priors, row_order, table, table_t, lag_cos, lag_sin, phases, m_buf, pg_buf, zm, zpg, a_s, b_s, mix, prior_own, prior_guest, u_s, v_s, sums, flow_send, flow_recv, grid_send, grid_recv,
     local_sem, send_x, recv_x, send_r, recv_r, send_p, recv_p, send_c, recv_c,
 ):
     gz, row, col = lax.axis_index("gz"), lax.axis_index("row"), lax.axis_index("col")
@@ -123,6 +123,15 @@
     own_p = pltpu.make_async_copy(sections.at[1 - x_lo], p_buf.at[body, pl.ds(128, 512)], local_sem.at[1])
     own_m.start()
     own_p.start()
+    constants = [
+        pltpu.make_async_copy(src, dst, local_sem.at[2 + k])
+        for k, (src, dst) in enumerate([
+            (priors_h, priors), (phases_h, phases), (table_h, table), (table_t_h, table_t),
+            (lag_cos_h, lag_cos), (lag_sin_h, lag_sin), (row_order_h, row_order),
+        ])
+    ]
+    for copy in constants:
+        copy.start()
 
     peers_plane = [(lax.rem(gz + dg, n_gz), row, lax.rem(col + dc, n_col)) for dg in range(n_gz) for dc in range(n_col) if dg or dc]
     peers_column = [(gz, lax.rem(row + d, n_row), col) for d in range(1, n_row)]
@@ -130,6 +139,7 @@
     for peer in peers_plane + peers_column:
         pl.semaphore_signal(barrier, inc=1, device_id=peer, device_id_type=MESH)
 
+    constants[0].wait()
     for c in range(2):
         for ii in range(2):
             for jj in range(2):
@@ -257,6 +267,8 @@
     send_rows(11)
     landing(10).wait_recv()
 
+    for copy in constants[1:]:
+        copy.wait()
     freq, off_u, off_v, mask_v = phases[0:1, :], phases[1:2, :], phases[2:3, :], phases[3:4, :]
     for t in range(2):
         value = prior_own[0] if t == 0 else prior_guest[...]
@@ -269,18 +281,8 @@
             jnp.cos(((turn + off_v) & (PATCH - 1)).astype(F32) * scale) * mask_v.astype(F32) * sign.astype(F32)
         )
 
-    arrive(0, mz_guest, has_in)
-    arrive(5)
-    arrive(1, mb_near)
-    arrive(2)
-    arrive(3)
-    arrive(7, mb_far, has_out)
-    arrive(4)
-    arrive(6)
-    arrive(8)
-    arrive(9)
-    for k in range(12):
-        guarded(k, functools.partial(wait_rows, k))
+    reach = (lax.broadcasted_iota(jnp.int32, (LAGS, LAGS), 0) - LAGS // 2).astype(F32)
+    unit = 1.0 / (512.0 * 512.0 * 512.0)
 
     def first_pass(src, dst, block):
         at = al(block * 256)
@@ -289,40 +291,89 @@
                 table[...], src[pl.ds(256 * i, 512), pl.ds(at, 256)], preferred_element_type=F32
             ).astype(BF16)
 
-    pl.loop(0, 5)(lambda b: first_pass(m_buf, zm, b))
-    pl.loop(0, 3)(lambda b: first_pass(p_buf, zpg.at[0], b))
-    pl.loop(0, 3)(lambda b: first_pass(g_buf, zpg.at[1], b))
-
-    reach = (lax.broadcasted_iota(jnp.int32, (LAGS, LAGS), 0) - LAGS // 2).astype(F32)
-    unit = 1.0 / (512.0 * 512.0 * 512.0)
+    def rows_in(*ks):
+        for k in ks:
+            guarded(k, functools.partial(wait_rows, k))
 
     def lag_table(r):
         return (lag_cos[...] * u_s[pl.ds(r, 1), :] + lag_sin[...] * v_s[pl.ds(r, 1), :]).astype(BF16)
 
-    @pl.loop(0, 8)
-    def _(n):
-        t = n // 4
-        i = (n // 2) % 2
-        j = n % 2
-        tile = x_lo + t * (1 - 2 * x_lo)
-        at_m = al((tile * 2 + j) * 256)
-        at_x = al(j * 256)
-        a_s[...] = jnp.dot(zm[i, :, pl.ds(at_m, 512)], table_t[...], preferred_element_type=F32)
-        b_s[...] = jnp.dot(zpg[t, i, :, pl.ds(at_x, 512)], table_t[...], preferred_element_type=F32)
-
-        @pl.loop(0, 8)
-        def _(rc):
-            for kb in range(2):
+    def pairs(t, j, between=None):
+        tile = x_lo if t == 0 else 1 - x_lo
+        at_m, at_x = al((tile * 2 + j) * 256), al(j * 256)
+
+        def spectra(h):
+            i, kb = h // 2, h % 2
+            rows = pl.ds(kb * 256, 256)
+            a_s[h % 2] = jnp.dot(zm[i, rows, pl.ds(at_m, 512)], table_t[...], preferred_element_type=F32)
+            b_s[h % 2] = jnp.dot(zpg[t, i, rows, pl.ds(at_x, 512)], table_t[...], preferred_element_type=F32)
+
+        def products(h):
+            for rc in range(8):
                 for lb in range(2):
-                    cross_chunk(a_s, b_s, mix, kb, lb, rc)
-
-        rows = lag_table(8 * t + i * 2 + j)
-        columns = lag_table(8 * t + 4 + i * 2 + j)
-        half = jnp.dot(rows, mix[...], preferred_element_type=F32).astype(BF16)
-        surface = lax.dot_general(half, columns, (((1,), (1,)), ((), ())), preferred_element_type=F32) * unit
-        weights = surface * surface
-        sums[0, pl.ds(n, 1), :] = jnp.sum(weights, axis=0, keepdims=True)
-        sums[1, pl.ds(n, 1), :] = jnp.sum(weights * reach, axis=0, keepdims=True)
+                    cross_chunk(a_s.at[h % 2], b_s.at[h % 2], mix.at[h // 2], h % 2, lb, rc)
+
+        def window(i):
+            n = t * 4 + i * 2 + j
+            rows = lag_table(8 * t + i * 2 + j)
+            columns = lag_table(8 * t + 4 + i * 2 + j)
+            half = jnp.dot(rows, mix[i], preferred_element_type=F32).astype(BF16)
+            surface = lax.dot_general(half, columns, (((1,), (1,)), ((), ())), preferred_element_type=F32) * unit
+            weights = surface * surface
+            sums[0, pl.ds(n, 1), :] = jnp.sum(weights, axis=0, keepdims=True)
+            sums[1, pl.ds(n, 1), :] = jnp.sum(weights * reach, axis=0, keepdims=True)
+
+        spectra(0)
+        spectra(1)
+        products(0)
+        spectra(2)
+        products(1)
+        if between is not None:
+            between()
+        spectra(3)
+        window(0)
+        products(2)
+        products(3)
+        window(1)
+
+    rows_in(10, 11)
+    first_pass(m_buf, zm, 1 + 2 * x_lo)
+    first_pass(p_buf, zpg.at[0], 1)
+    arrive(0, mz_guest, has_in)
+    arrive(5)
+    arrive(1, mb_near)
+    rows_in(0, 5)
+    first_pass(m_buf, zm, 4 - 4 * x_lo)
+    arrive(7, mb_far, has_out)
+    rows_in(1)
+    first_pass(m_buf, zm, 2)
+    arrive(2)
+    rows_in(7)
+    first_pass(m_buf, zm, 4 * x_lo)
+    rows_in(2)
+    first_pass(p_buf, zpg.at[0], 2 - 2 * x_lo)
+
+    def arrivals():
+        arrive(3)
+        arrive(6)
+
+    pairs(0, 1 - x_lo, arrivals)
+    rows_in(3)
+    first_pass(p_buf, zpg.at[0], 2 * x_lo)
+    rows_in(6)
+    first_pass(g_buf, zpg.at[1], 1)
+    pairs(0, x_lo)
+    arrive(4)
+    arrive(8)
+    arrive(9)
+    rows_in(4)
+    first_pass(m_buf, zm, 3 - 2 * x_lo)
+    rows_in(8)
+    first_pass(g_buf, zpg.at[1], 2 * x_lo)
+    pairs(1, x_lo)
+    rows_in(9)
+    first_pass(g_buf, zpg.at[1], 2 - 2 * x_lo)
+    pairs(1, 1 - x_lo)
 
     lane = lax.broadcasted_iota(jnp.int32, (8, 128), 1)
     along = (lane - LAGS // 2).astype(F32)
@@ -418,21 +469,27 @@
     table = forward_table()
     lag_cos, lag_sin = lag_tables()
     vmem = pl.BlockSpec(memory_space=pltpu.VMEM)
-    smem = pl.BlockSpec(memory_space=pltpu.SMEM)
     dma = pltpu.SemaphoreType.DMA
     return pl.pallas_call(
         kernel,
         out_shape=jax.ShapeDtypeStruct((2, 128), F32),
-        in_specs=[pl.BlockSpec(memory_space=pl.ANY), smem, smem, vmem, vmem, vmem, vmem, vmem],
+        in_specs=[pl.BlockSpec(memory_space=pltpu.HBM)] * 8,
         out_specs=vmem,
         scratch_shapes=[
+            pltpu.SMEM((2, 2, 2, 2), jnp.int32),
+            pltpu.SMEM((16,), jnp.int32),
+            pltpu.VMEM((512, 512), BF16),
+            pltpu.VMEM((512, 512), BF16),
+            pltpu.VMEM((LAGS, 512), F32),
+            pltpu.VMEM((LAGS, 512), F32),
+            pltpu.VMEM((8, 512), jnp.int32),
             pltpu.VMEM((768, 1280), BF16),
             pltpu.VMEM((2, 768, 768), BF16),
             pltpu.VMEM((2, 512, 1280), BF16),
             pltpu.VMEM((2, 2, 512, 768), BF16),
-            pltpu.VMEM((512, 512), F32),
-            pltpu.VMEM((512, 512), F32),
-            pltpu.VMEM((512, 512), BF16),
+            pltpu.VMEM((2, 256, 512), F32),
+            pltpu.VMEM((2, 256, 512), F32),
+            pltpu.VMEM((2, 512, 512), BF16),
             pltpu.VMEM((2, 8, 128), jnp.int32),
             pltpu.VMEM((8, 128), jnp.int32),
             pltpu.VMEM((16, 512), F32),
@@ -442,7 +499,7 @@
             pltpu.VMEM((16, 2, 128), F32),
             pltpu.VMEM((2, 128), F32),
             pltpu.VMEM((8, 2, 128), F32),
-            dma((2,)),
+            dma((9,)),
             dma((11,)),
             dma((11,)),
             dma((24,)),
@@ -452,7 +509,7 @@
             dma((7,)),
             dma((7,)),
         ],
-        compiler_params=pltpu.CompilerParams(collective_id=0, has_side_effects=True, vmem_limit_bytes=48 * 1024 * 1024),
+        compiler_params=pltpu.CompilerParams(collective_id=0, has_side_effects=True, vmem_limit_bytes=67_043_328),
     )(
         sections, priors, row_order, jnp.asarray(table), jnp.asarray(np.ascontiguousarray(table.T)),
         jnp.asarray(lag_cos), jnp.asarray(lag_sin), jnp.asarray(phase_rows()),

time: 66.3 us -> 51.3 us (0.77)
  Pallas kernels: 58 us -> 49.9 us
  local copies, waits for them, and re-layouts: 7.83 us -> 1.24 us
    pallas_call x1, Pallas kernels: 58 us -> 49.9 us  [body(): pl.pallas_call(kernel, out_shape=jax.ShapeDtypeStruct((2, 128), F32), in_...]
    unnamed x17 -> x1, local copies, waits for them, and re-layouts: 7.83 us -> 1.24 us
where the time goes in v2:
time: 51.3 us; the launch traced here: 51.1 us
  Pallas kernels  49.9 us (97%)
  local copies, waits for them, and re-layouts  1.24 us (2%)
    pallas_call x1, Pallas kernels, body(): pl.pallas_call(kernel, out_shape=jax.ShapeDtypeStruct((2, 128), F32), in_...  49.9 us
    unnamed x1, local copies, waits for them, and re-layouts  1.24 us

profile of v2, /device:TPU:1, one launch (start us, length us, event | category | flops | bytes accessed | tf_op | source)
XLA Modules:
  0.0 51.1 jit_solution(7500252417973018176)
XLA Ops:
  0.0 49.9 %shard_map.82 = f32[2,128]{1,0:T(2,128)} custom-call(bf16[2,512,512]{2,1,0:T(8,128)(2,1)} %sections.1, s32[2,2,2,2]{3,2,1,0:T(2,128)} %priors_h.1, s32[16]{0:T(128)} %row_order_h.1, bf16[512,512]{1,0:T(8,128)(2,1)} %constant.10.clone.table_h, bf16[512,512]{1,0:T(8,128)(2,1)} %constant.11.clone.table_t_h, f32[128,512]{1,0:T(8,128)} %constant.12.clone.lag_cos_h, ...), custom_call_target="tpu_custom_call" | custom-call | tf_op jit(solution)/shard_map/pallas_call | solution.py:473
  49.9 1.2 %copy.10 = f32[2,128]{1,0:T(2,128)} copy(f32[2,128]{1,0:T(2,128)} %shard_map.82) | data formatting | bytes 2048

commit v3 on v2

--- a/solution.py
+++ b/solution.py
@@ -87,8 +87,8 @@
 
 def kernel(
     sections, priors_h, row_order_h, table_h, table_t_h, lag_cos_h, lag_sin_h, phases_h, out,
-    priors, row_order, table, table_t, lag_cos, lag_sin, phases, m_buf, pg_buf, zm, zpg, a_s, b_s, mix, prior_own, prior_guest, u_s, v_s, sums, flow_send, flow_recv, grid_send, grid_recv,
-    local_sem, send_x, recv_x, send_r, recv_r, send_p, recv_p, send_c, recv_c,
+    priors, row_order, table, table_t, lag_cos, lag_sin, phases, m_buf, pg_buf, zm, zpg, a_s, b_s, mix, prior_own, prior_guest, u_s, v_s, sums, flow_send, flow_recv, known,
+    local_sem, send_x, recv_x, send_r, recv_r, send_f, recv_f,
 ):
     gz, row, col = lax.axis_index("gz"), lax.axis_index("row"), lax.axis_index("col")
     n_gz, n_row, n_col = lax.axis_size("gz"), lax.axis_size("row"), lax.axis_size("col")
@@ -133,11 +133,29 @@
     for copy in constants:
         copy.start()
 
-    peers_plane = [(lax.rem(gz + dg, n_gz), row, lax.rem(col + dc, n_col)) for dg in range(n_gz) for dc in range(n_col) if dg or dc]
-    peers_column = [(gz, lax.rem(row + d, n_row), col) for d in range(1, n_row)]
+    def at(dg, dr, dc):
+        return (lax.rem(gz + dg, n_gz), lax.rem(row + dr, n_row), lax.rem(col + dc, n_col))
+
+    z_ring = [at(0, 0, 2), at(0, 0, n_col - 2)]
+    row_ring = [at(0, 1, 0), at(0, n_row - 1, 0)]
+    near_peers = [a_id, b_id, (gz, row, lax.rem(col + side + n_col, n_col))] + z_ring + row_ring
     barrier = pltpu.get_barrier_semaphore()
-    for peer in peers_plane + peers_column:
+    for peer in near_peers:
         pl.semaphore_signal(barrier, inc=1, device_id=peer, device_id_type=MESH)
+
+    rounds = [
+        near_peers,
+        [a_id, b_id, (1 - gz, row, col)],
+        z_ring + [at(0, 0, n_col // 2)],
+        [at(0, 2, 0), at(0, n_row - 2, 0)],
+    ]
+
+    def tell(k):
+        for peer in rounds[k]:
+            pl.semaphore_signal(known.at[k], inc=1, device_id=peer, device_id_type=MESH)
+
+    def hear(k):
+        pl.semaphore_wait(known.at[k], len(rounds[k]))
 
     constants[0].wait()
     for c in range(2):
@@ -169,7 +187,8 @@
 
     own_m.wait()
     own_p.wait()
-    pl.semaphore_wait(barrier, len(peers_plane) + len(peers_column))
+    pl.semaphore_wait(barrier, len(near_peers))
+    tell(0)
 
     def remote(k, src, dst, device):
         return pltpu.make_async_remote_copy(
@@ -341,10 +360,14 @@
     first_pass(p_buf, zpg.at[0], 1)
     arrive(0, mz_guest, has_in)
     arrive(5)
+    hear(0)
+    tell(1)
     arrive(1, mb_near)
     rows_in(0, 5)
     first_pass(m_buf, zm, 4 - 4 * x_lo)
     arrive(7, mb_far, has_out)
+    hear(1)
+    tell(2)
     rows_in(1)
     first_pass(m_buf, zm, 2)
     arrive(2)
@@ -357,7 +380,10 @@
         arrive(3)
         arrive(6)
 
+    hear(2)
+    tell(3)
     pairs(0, 1 - x_lo, arrivals)
+    hear(3)
     rows_in(3)
     first_pass(p_buf, zpg.at[0], 2 * x_lo)
     rows_in(6)
@@ -399,54 +425,30 @@
                 line = line + jnp.where(lane1 == place, flow_r, 0.0) + jnp.where(lane1 == place + 64, flow_c, 0.0)
         flow_send[i : i + 1, :] = line
 
-    me_plane = gz * n_col + col
-
-    def to_plane(d, peer):
-        return pltpu.make_async_remote_copy(
-            src_ref=flow_send, dst_ref=flow_recv.at[me_plane], send_sem=send_p.at[d], recv_sem=recv_p.at[d],
-            device_id=peer, device_id_type=MESH,
-        )
-
-    offsets = [(dg, dc) for dg in range(n_gz) for dc in range(n_col) if dg or dc]
-    for d, peer in enumerate(peers_plane):
-        to_plane(d, peer).start()
-    lines = flow_send[...]
-    for d, (dg, dc) in enumerate(offsets):
-        source = lax.rem(gz + n_gz - dg, n_gz) * n_col + lax.rem(col + n_col - dc, n_col)
-        pltpu.make_async_remote_copy(
-            src_ref=flow_recv.at[source], dst_ref=flow_recv.at[source], send_sem=send_p.at[d], recv_sem=recv_p.at[d],
-            device_id=a_id, device_id_type=MESH,
-        ).wait_recv()
-        lines = lines + flow_recv[source]
-    grid_send[...] = lines
-
-    def to_column(d, peer):
-        return pltpu.make_async_remote_copy(
-            src_ref=grid_send, dst_ref=grid_recv.at[row], send_sem=send_c.at[d], recv_sem=recv_c.at[d],
-            device_id=peer, device_id_type=MESH,
-        )
-
-    for d, peer in enumerate(peers_column):
-        to_column(d, peer).start()
+    n_all = n_gz * n_row * n_col
+    me = (gz * n_row + row) * n_col + col
+    for dg in range(n_gz):
+        for dr in range(n_row):
+            for dc in range(n_col):
+                if dg or dr or dc:
+                    pltpu.make_async_remote_copy(
+                        src_ref=flow_send, dst_ref=flow_recv.at[me], send_sem=send_f, recv_sem=recv_f,
+                        device_id=at(dg, dr, dc), device_id_type=MESH,
+                    ).start()
     want = [row_order[2 * row + m] for m in range(2)]
     picked = [jnp.zeros((1, 128), F32) for _ in range(2)]
-
-    def pick(block, owner):
+    others = flow_recv.at[pl.ds(0, n_all - 1)]
+    pltpu.make_async_copy(others, others, recv_f).wait()
+    flow_recv[pl.ds(me, 1)] = flow_send[...][None]
+    for r in range(n_row):
+        block = sum(jnp.sum(flow_recv[pl.ds((g * n_row + r) * n_col, n_col)], axis=0) for g in range(n_gz))
         for m in range(2):
             for i in range(2):
-                hit = jnp.full((1, 128), want[m], jnp.int32) == jnp.full((1, 128), 2 * owner + i, jnp.int32)
+                hit = jnp.full((1, 128), want[m], jnp.int32) == 2 * r + i
                 picked[m] = picked[m] + jnp.where(hit, block[i : i + 1, :], 0.0)
-
-    pick(lines, row)
-    for d in range(n_row - 1):
-        source = lax.rem(row + n_row - (d + 1), n_row)
-        pltpu.make_async_remote_copy(
-            src_ref=grid_recv.at[source], dst_ref=grid_recv.at[source], send_sem=send_c.at[d], recv_sem=recv_c.at[d],
-            device_id=a_id, device_id_type=MESH,
-        ).wait_recv()
-        pick(grid_recv[source], source)
     for m in range(2):
         out[m : m + 1, :] = picked[m]
+    pltpu.make_async_copy(others, others, send_f).wait()
 
     sends = [
         (pa_outer, None), (pa_near, None), (m_a, None), (m_n, has_out), (pa_mid, None), (mz_own, has_out), (mb_tile, None),
@@ -459,10 +461,6 @@
             pl.when(cond)(copy.wait_send)
     for k in range(12):
         guarded(k, functools.partial(wait_sent_rows, k))
-    for d, peer in enumerate(peers_plane):
-        to_plane(d, peer).wait_send()
-    for d, peer in enumerate(peers_column):
-        to_column(d, peer).wait_send()
 
 
 def body(sections, priors, row_order):
@@ -496,18 +494,15 @@
             pltpu.VMEM((16, 512), F32),
             pltpu.VMEM((2, 8, 128), F32),
             pltpu.VMEM((2, 128), F32),
-            pltpu.VMEM((16, 2, 128), F32),
-            pltpu.VMEM((2, 128), F32),
-            pltpu.VMEM((8, 2, 128), F32),
+            pltpu.VMEM((128, 2, 128), F32),
+            pltpu.SemaphoreType.REGULAR((4,)),
             dma((9,)),
             dma((11,)),
             dma((11,)),
             dma((24,)),
             dma((24,)),
-            dma((15,)),
-            dma((15,)),
-            dma((7,)),
-            dma((7,)),
+            dma,
+            dma,
         ],
         compiler_params=pltpu.CompilerParams(collective_id=0, has_side_effects=True, vmem_limit_bytes=67_043_328),
     )(

time: 51.3 us -> 48.1 us (0.938)
  Pallas kernels: 49.9 us -> 46.7 us
    pallas_call x1, Pallas kernels: 49.9 us -> 46.7 us  [body(): pl.pallas_call(kernel, out_shape=jax.ShapeDtypeStruct((2, 128), F32), in_...]
where the time goes in v3:
time: 48.1 us; the launch traced here: 47.9 us
  Pallas kernels  46.7 us (97%)
  local copies, waits for them, and re-layouts  1.24 us (3%)
    pallas_call x1, Pallas kernels, body(): pl.pallas_call(kernel, out_shape=jax.ShapeDtypeStruct((2, 128), F32), in_...  46.7 us
    unnamed x1, local copies, waits for them, and re-layouts  1.24 us

profile of v3, /device:TPU:1, one launch (start us, length us, event | category | flops | bytes accessed | tf_op | source)
XLA Modules:
  0.0 47.9 jit_solution(11297546640141356005)
XLA Ops:
  0.0 46.7 %shard_map.82 = f32[2,128]{1,0:T(2,128)} custom-call(bf16[2,512,512]{2,1,0:T(8,128)(2,1)} %sections.1, s32[2,2,2,2]{3,2,1,0:T(2,128)} %priors_h.1, s32[16]{0:T(128)} %row_order_h.1, bf16[512,512]{1,0:T(8,128)(2,1)} %constant.10.clone.table_h, bf16[512,512]{1,0:T(8,128)(2,1)} %constant.11.clone.table_t_h, f32[128,512]{1,0:T(8,128)} %constant.12.clone.lag_cos_h, ...), custom_call_target="tpu_custom_call" | custom-call | tf_op jit(solution)/shard_map/pallas_call | solution.py:471
  46.7 1.2 %copy.10 = f32[2,128]{1,0:T(2,128)} copy(f32[2,128]{1,0:T(2,128)} %shard_map.82) | data formatting | bytes 2048

commit v4 on v3

--- a/solution.py
+++ b/solution.py
@@ -87,7 +87,7 @@
 
 def kernel(
     sections, priors_h, row_order_h, table_h, table_t_h, lag_cos_h, lag_sin_h, phases_h, out,
-    priors, row_order, table, table_t, lag_cos, lag_sin, phases, m_buf, pg_buf, zm, zpg, a_s, b_s, mix, prior_own, prior_guest, u_s, v_s, sums, flow_send, flow_recv, known,
+    priors, row_order, table, table_t, lag_cos, lag_sin, phases, m_buf, pg_buf, zm, zpg, a_s, b_s, mix, prior_own, prior_guest, u_s, v_s, lag_s, sums, flow_send, flow_recv, known,
     local_sem, send_x, recv_x, send_r, recv_r, send_f, recv_f,
 ):
     gz, row, col = lax.axis_index("gz"), lax.axis_index("row"), lax.axis_index("col")
@@ -138,7 +138,7 @@
 
     z_ring = [at(0, 0, 2), at(0, 0, n_col - 2)]
     row_ring = [at(0, 1, 0), at(0, n_row - 1, 0)]
-    near_peers = [a_id, b_id, (gz, row, lax.rem(col + side + n_col, n_col))] + z_ring + row_ring
+    near_peers = [a_id, b_id] + z_ring + row_ring
     barrier = pltpu.get_barrier_semaphore()
     for peer in near_peers:
         pl.semaphore_signal(barrier, inc=1, device_id=peer, device_id_type=MESH)
@@ -190,115 +190,128 @@
     pl.semaphore_wait(barrier, len(near_peers))
     tell(0)
 
-    def remote(k, src, dst, device):
+    spans = (pl.ds(128, 128), pl.ds(512, 128), pl.ds(256, 256))
+
+    def part(k, p, src, src_at, dst, dst_at, width, device):
         return pltpu.make_async_remote_copy(
-            src_ref=src, dst_ref=dst, send_sem=send_x.at[k], recv_sem=recv_x.at[k], device_id=device, device_id_type=MESH
+            src_ref=src.at[spans[p], pl.ds(src_at, width)], dst_ref=dst.at[spans[p], pl.ds(dst_at, width)],
+            send_sem=send_x.at[3 * k + p], recv_sem=recv_x.at[3 * k + p], device_id=device, device_id_type=MESH,
         )
 
-    def strip(ref, start, width=128):
-        return ref.at[body, pl.ds(start, width)]
-
-    pa_outer = remote(0, strip(p_buf, outer_p), strip(m_buf, outer), a_id)
-    pa_near = remote(1, strip(p_buf, near_p), strip(m_buf, near), a_id)
-    m_a = remote(2, strip(m_buf, near), strip(p_buf, side_out), a_id)
-    m_n = remote(3, strip(m_buf, outer), strip(p_buf, side_in), n_id)
-    pa_mid = remote(4, strip(p_buf, 256, 256), strip(m_buf, al(c0 + 128), 256), a_id)
-    mz_own = remote(5, strip(m_buf, outer), strip(m_buf, m_far_in), z_out)
-    mb_tile = remote(6, strip(m_buf, c0, 512), strip(g_buf, 128, 512), b_id)
-    mz_guest = remote(7, strip(m_buf, outer_g), strip(m_buf, m_far_out), z_in)
-    mb_near = remote(8, strip(m_buf, near_g), strip(g_buf, side_in), b_id)
-    mb_far = remote(9, strip(m_buf, m_far_out), strip(g_buf, side_out), b_id)
-    prior_id = (gz + x_lo * (1 - 2 * gz), row, col - side)
-    prior_send = remote(10, prior_own.at[1], prior_guest, prior_id)
-
-    prior_send.start()
-    pa_outer.start()
-    mb_tile.start()
-    pl.when(has_out)(mz_own.start)
-    pa_near.start()
-    m_a.start()
-    pl.when(has_out)(m_n.start)
-    pa_mid.start()
-
+    sent = {
+        0: (p_buf, outer_p, m_buf, outer, 128, a_id),
+        1: (p_buf, near_p, m_buf, near, 128, a_id),
+        2: (m_buf, near, p_buf, side_out, 128, a_id),
+        3: (m_buf, outer, p_buf, side_in, 128, n_id),
+        4: (p_buf, 256, m_buf, al(c0 + 128), 256, a_id),
+        5: (m_buf, outer, m_buf, m_far_in, 128, z_out),
+        6: (m_buf, c0, g_buf, 128, 512, b_id),
+        7: (m_buf, outer_g, m_buf, m_far_out, 128, z_in),
+        8: (m_buf, near_g, g_buf, side_in, 128, b_id),
+        9: (m_buf, m_far_out, g_buf, side_out, 128, b_id),
+        10: (m_buf, c0, g_buf, 128, 256, b_id),
+        11: (m_buf, al(c0 + 256), g_buf, 384, 256, b_id),
+    }
     landed = {
-        0: strip(m_buf, outer_g), 1: strip(m_buf, near_g), 2: strip(p_buf, side_in), 3: strip(p_buf, side_out),
-        4: strip(m_buf, al(c1 + 128), 256), 5: strip(m_buf, m_far_in), 6: strip(g_buf, 128, 512), 7: strip(m_buf, m_far_out),
-        8: strip(g_buf, side_out), 9: strip(g_buf, side_in), 10: prior_guest,
-    }
-    when_recv = {3: has_out, 5: has_in, 7: has_out, 9: has_in}
-
-    def landing(k):
-        ref = landed[k]
-        return remote(k, ref, ref, a_id)
-
-    def rows_of(k, ref, start, width):
-        cols = pl.ds(start, width)
-        up = pltpu.make_async_remote_copy(
-            src_ref=ref.at[pl.ds(128, 128), cols], dst_ref=ref.at[pl.ds(640, 128), cols],
-            send_sem=send_r.at[2 * k], recv_sem=recv_r.at[2 * k], device_id=up_id, device_id_type=MESH,
-        )
-        down = pltpu.make_async_remote_copy(
-            src_ref=ref.at[pl.ds(512, 128), cols], dst_ref=ref.at[pl.ds(0, 128), cols],
-            send_sem=send_r.at[2 * k + 1], recv_sem=recv_r.at[2 * k + 1], device_id=down_id, device_id_type=MESH,
-        )
-        return up, down
-
-    pieces = {
         0: (m_buf, outer_g, 128), 1: (m_buf, near_g, 128), 2: (p_buf, side_in, 128), 3: (p_buf, side_out, 128),
         4: (m_buf, al(c1 + 128), 256), 5: (m_buf, m_far_in, 128), 6: (g_buf, 128, 512), 7: (m_buf, m_far_out, 128),
-        8: (g_buf, side_out, 128), 9: (g_buf, side_in, 128), 10: (m_buf, c0, 512), 11: (p_buf, 128, 512),
+        8: (g_buf, side_out, 128), 9: (g_buf, side_in, 128), 10: (g_buf, 128, 256), 11: (g_buf, 384, 256),
     }
-
-    def send_rows(k):
-        up, down = rows_of(k, *pieces[k])
-        pl.when(has_up)(up.start)
-        pl.when(has_down)(down.start)
-
-    def wait_rows(k):
-        up, down = rows_of(k, *pieces[k])
-        pl.when(has_down)(up.wait_recv)
-        pl.when(has_up)(down.wait_recv)
-
-    def wait_sent_rows(k):
-        up, down = rows_of(k, *pieces[k])
-        pl.when(has_up)(up.wait_send)
-        pl.when(has_down)(down.wait_send)
-
-    def guarded(k, do):
-        if k in when_recv:
-            pl.when(when_recv[k])(do)
+    parts_of = {k: (0, 1, 2) for k in range(10)}
+    parts_of.update({6: (0, 1), 10: (2,), 11: (2,)})
+    when_send = {3: has_out, 5: has_out, 7: has_in, 9: has_out}
+    when_recv = {3: has_out, 5: has_in, 7: has_out, 9: has_in}
+
+    def guarded(conds, k, do):
+        if k in conds:
+            pl.when(conds[k])(do)
         else:
             do()
 
-    def arrive(k, forward=None, cond=None):
+    def send(k, *parts):
         def do():
-            landing(k).wait_recv()
-            send_rows(k)
-
-        guarded(k, do)
+            for p in parts:
+                part(k, p, *sent[k]).start()
+
+        guarded(when_send, k, do)
+
+    def land(k, p):
+        ref, start, width = landed[k]
+        part(k, p, ref, start, ref, start, width, a_id).wait_recv()
+
+    pieces = dict(landed)
+    pieces.update({10: (m_buf, c0, 512), 11: (p_buf, 128, 512)})
+
+    def row_copy(k, down):
+        ref, start, width = pieces[k]
+        cols = pl.ds(start, width)
+        src, dst = (pl.ds(512, 128), pl.ds(0, 128)) if down else (pl.ds(128, 128), pl.ds(640, 128))
+        return pltpu.make_async_remote_copy(
+            src_ref=ref.at[src, cols], dst_ref=ref.at[dst, cols], send_sem=send_r.at[2 * k + down],
+            recv_sem=recv_r.at[2 * k + down], device_id=down_id if down else up_id, device_id_type=MESH,
+        )
+
+    def send_row(k, down):
+        pl.when(has_down if down else has_up)(row_copy(k, down).start)
+
+    def edges(k, forward=None):
+        def do():
+            for p in range(2):
+                land(k, p)
+                send_row(k, p)
+
+        guarded(when_recv, k, do)
         if forward is not None:
-            if cond is None:
-                forward.start()
-            else:
-                pl.when(cond)(forward.start)
-
-    send_rows(10)
-    send_rows(11)
-    landing(10).wait_recv()
+            send(forward, 0, 1)
+
+    def centre(k, forward=None):
+        guarded(when_recv, k, lambda: land(k, 2))
+        if forward is not None:
+            send(forward, 2)
+
+    def rows_in(*ks):
+        def do(k):
+            pl.when(has_down)(row_copy(k, 0).wait_recv)
+            pl.when(has_up)(row_copy(k, 1).wait_recv)
+
+        for k in ks:
+            guarded(when_recv, k, functools.partial(do, k))
+
+    prior_id = (gz + x_lo * (1 - 2 * gz), row, col - side)
+    prior_send = pltpu.make_async_remote_copy(
+        src_ref=prior_own.at[1], dst_ref=prior_guest, send_sem=send_x.at[36], recv_sem=recv_x.at[36],
+        device_id=prior_id, device_id_type=MESH,
+    )
+
+    send(0, 0, 1)
+    send(6, 0, 1)
+    send(5, 0, 1)
+    send(0, 2)
+    send(1, 0, 1)
+    send(5, 2)
+    send(1, 2)
+    send(10, 2)
+    send(2, 0, 1, 2)
+    prior_send.start()
+    for k in (10, 11):
+        for down in range(2):
+            send_row(k, down)
 
     for copy in constants[1:]:
         copy.wait()
     freq, off_u, off_v, mask_v = phases[0:1, :], phases[1:2, :], phases[2:3, :], phases[3:4, :]
-    for t in range(2):
+
+    def lag_tables_of(t):
         value = prior_own[0] if t == 0 else prior_guest[...]
         sign = (1 - 2 * x_lo) * (1 - 2 * t)
-        wide = jnp.concatenate([value] * 4, axis=1) * sign
-        turn = wide * freq
+        turn = jnp.concatenate([value] * 4, axis=1) * sign * freq
         scale = 2.0 * np.pi / PATCH
-        u_s[8 * t : 8 * t + 8, :] = jnp.cos(((turn + off_u) & (PATCH - 1)).astype(F32) * scale)
-        v_s[8 * t : 8 * t + 8, :] = (
-            jnp.cos(((turn + off_v) & (PATCH - 1)).astype(F32) * scale) * mask_v.astype(F32) * sign.astype(F32)
-        )
+        u_s[...] = jnp.cos(((turn + off_u) & (PATCH - 1)).astype(F32) * scale)
+        v_s[...] = jnp.cos(((turn + off_v) & (PATCH - 1)).astype(F32) * scale) * mask_v.astype(F32) * sign.astype(F32)
+
+        @pl.loop(0, 8)
+        def _(r):
+            lag_s[8 * t + r] = (lag_cos[...] * u_s[pl.ds(r, 1), :] + lag_sin[...] * v_s[pl.ds(r, 1), :]).astype(BF16)
 
     reach = (lax.broadcasted_iota(jnp.int32, (LAGS, LAGS), 0) - LAGS // 2).astype(F32)
     unit = 1.0 / (512.0 * 512.0 * 512.0)
@@ -310,34 +323,27 @@
                 table[...], src[pl.ds(256 * i, 512), pl.ds(at, 256)], preferred_element_type=F32
             ).astype(BF16)
 
-    def rows_in(*ks):
-        for k in ks:
-            guarded(k, functools.partial(wait_rows, k))
-
-    def lag_table(r):
-        return (lag_cos[...] * u_s[pl.ds(r, 1), :] + lag_sin[...] * v_s[pl.ds(r, 1), :]).astype(BF16)
-
-    def pairs(t, j, between=None):
+    def pairs(t, j, between=None, b_done=False):
         tile = x_lo if t == 0 else 1 - x_lo
-        at_m, at_x = al((tile * 2 + j) * 256), al(j * 256)
+        at_m = al((tile * 2 + j) * 256)
 
         def spectra(h):
             i, kb = h // 2, h % 2
-            rows = pl.ds(kb * 256, 256)
-            a_s[h % 2] = jnp.dot(zm[i, rows, pl.ds(at_m, 512)], table_t[...], preferred_element_type=F32)
-            b_s[h % 2] = jnp.dot(zpg[t, i, rows, pl.ds(at_x, 512)], table_t[...], preferred_element_type=F32)
+            a_s[h % 2] = jnp.dot(zm[i, pl.ds(kb * 256, 256), pl.ds(at_m, 512)], table_t[...], preferred_element_type=F32)
+            if not b_done:
+                spectra_b(t, j, h)
 
         def products(h):
             for rc in range(8):
                 for lb in range(2):
-                    cross_chunk(a_s.at[h % 2], b_s.at[h % 2], mix.at[h // 2], h % 2, lb, rc)
+                    cross_chunk(a_s.at[h % 2], b_s.at[h], mix.at[h // 2], h % 2, lb, rc)
 
         def window(i):
             n = t * 4 + i * 2 + j
-            rows = lag_table(8 * t + i * 2 + j)
-            columns = lag_table(8 * t + 4 + i * 2 + j)
-            half = jnp.dot(rows, mix[i], preferred_element_type=F32).astype(BF16)
-            surface = lax.dot_general(half, columns, (((1,), (1,)), ((), ())), preferred_element_type=F32) * unit
+            half = jnp.dot(lag_s[8 * t + i * 2 + j], mix[i], preferred_element_type=F32).astype(BF16)
+            surface = unit * lax.dot_general(
+                half, lag_s[8 * t + 4 + i * 2 + j], (((1,), (1,)), ((), ())), preferred_element_type=F32
+            )
             weights = surface * surface
             sums[0, pl.ds(n, 1), :] = jnp.sum(weights, axis=0, keepdims=True)
             sums[1, pl.ds(n, 1), :] = jnp.sum(weights * reach, axis=0, keepdims=True)
@@ -355,48 +361,73 @@
         products(3)
         window(1)
 
-    rows_in(10, 11)
+    def spectra_b(t, j, h):
+        b_s[h] = jnp.dot(
+            zpg[t, h // 2, pl.ds(h % 2 * 256, 256), pl.ds(al(j * 256), 512)], table_t[...], preferred_element_type=F32
+        )
+
+    hear(0)
+    send(3, 0, 1, 2)
+    send(4, 0, 1, 2)
+    tell(1)
+    lag_tables_of(0)
+    edges(0, 7)
+    rows_in(10)
     first_pass(m_buf, zm, 1 + 2 * x_lo)
+    centre(0, 7)
+    edges(5)
+    edges(1, 8)
+    edges(7, 9)
+    send(11, 2)
+    rows_in(11)
     first_pass(p_buf, zpg.at[0], 1)
-    arrive(0, mz_guest, has_in)
-    arrive(5)
-    hear(0)
-    tell(1)
-    arrive(1, mb_near)
+    centre(1, 8)
+    prior_send.wait_recv()
+    lag_tables_of(1)
+    centre(5)
     rows_in(0, 5)
     first_pass(m_buf, zm, 4 - 4 * x_lo)
-    arrive(7, mb_far, has_out)
+    centre(7, 9)
     hear(1)
     tell(2)
     rows_in(1)
     first_pass(m_buf, zm, 2)
-    arrive(2)
+    edges(2)
     rows_in(7)
     first_pass(m_buf, zm, 4 * x_lo)
+    centre(2)
     rows_in(2)
     first_pass(p_buf, zpg.at[0], 2 - 2 * x_lo)
-
-    def arrivals():
-        arrive(3)
-        arrive(6)
-
     hear(2)
     tell(3)
+
+    def arrivals():
+        edges(3)
+        edges(6)
+
     pairs(0, 1 - x_lo, arrivals)
     hear(3)
+    centre(3)
     rows_in(3)
     first_pass(p_buf, zpg.at[0], 2 * x_lo)
+    edges(8)
+    pairs(0, x_lo)
+    edges(9)
+    edges(4)
+    centre(10)
+    centre(11)
     rows_in(6)
     first_pass(g_buf, zpg.at[1], 1)
-    pairs(0, x_lo)
-    arrive(4)
-    arrive(8)
-    arrive(9)
+    centre(8)
+    rows_in(8)
+    first_pass(g_buf, zpg.at[1], 2 * x_lo)
+    for h in range(4):
+        spectra_b(1, x_lo, h)
+    centre(4)
     rows_in(4)
     first_pass(m_buf, zm, 3 - 2 * x_lo)
-    rows_in(8)
-    first_pass(g_buf, zpg.at[1], 2 * x_lo)
-    pairs(1, x_lo)
+    pairs(1, x_lo, b_done=True)
+    centre(9)
     rows_in(9)
     first_pass(g_buf, zpg.at[1], 2 - 2 * x_lo)
     pairs(1, 1 - x_lo)
@@ -450,17 +481,19 @@
         out[m : m + 1, :] = picked[m]
     pltpu.make_async_copy(others, others, send_f).wait()
 
-    sends = [
-        (pa_outer, None), (pa_near, None), (m_a, None), (m_n, has_out), (pa_mid, None), (mz_own, has_out), (mb_tile, None),
-        (mz_guest, has_in), (mb_near, None), (mb_far, has_out), (prior_send, None),
-    ]
-    for copy, cond in sends:
-        if cond is None:
-            copy.wait_send()
-        else:
-            pl.when(cond)(copy.wait_send)
+    prior_send.wait_send()
     for k in range(12):
-        guarded(k, functools.partial(wait_sent_rows, k))
+        def sent_all(k=k):
+            for p in parts_of[k]:
+                part(k, p, *sent[k]).wait_send()
+
+        guarded(when_send, k, sent_all)
+
+        def rows_sent(k=k):
+            pl.when(has_up)(row_copy(k, 0).wait_send)
+            pl.when(has_down)(row_copy(k, 1).wait_send)
+
+        guarded(when_recv, k, rows_sent)
 
 
 def body(sections, priors, row_order):
@@ -486,19 +519,20 @@
             pltpu.VMEM((2, 512, 1280), BF16),
             pltpu.VMEM((2, 2, 512, 768), BF16),
             pltpu.VMEM((2, 256, 512), F32),
-            pltpu.VMEM((2, 256, 512), F32),
+            pltpu.VMEM((4, 256, 512), F32),
             pltpu.VMEM((2, 512, 512), BF16),
             pltpu.VMEM((2, 8, 128), jnp.int32),
             pltpu.VMEM((8, 128), jnp.int32),
-            pltpu.VMEM((16, 512), F32),
-            pltpu.VMEM((16, 512), F32),
+            pltpu.VMEM((8, 512), F32),
+            pltpu.VMEM((8, 512), F32),
+            pltpu.VMEM((16, LAGS, 512), BF16),
             pltpu.VMEM((2, 8, 128), F32),
             pltpu.VMEM((2, 128), F32),
             pltpu.VMEM((128, 2, 128), F32),
             pltpu.SemaphoreType.REGULAR((4,)),
             dma((9,)),
-            dma((11,)),
-            dma((11,)),
+            dma((37,)),
+            dma((37,)),
             dma((24,)),
             dma((24,)),
             dma,

time: 48.1 us -> 46.3 us (0.963)
  Pallas kernels: 46.7 us -> 44.9 us
    pallas_call x1, Pallas kernels: 46.7 us -> 44.9 us  [body(): pl.pallas_call(kernel, out_shape=jax.ShapeDtypeStruct((2, 128), F32), in_...]
where the time goes in v4:
time: 46.3 us; the launch traced here: 46.2 us
  Pallas kernels  44.9 us (97%)
  local copies, waits for them, and re-layouts  1.24 us (3%)
    pallas_call x1, Pallas kernels, body(): pl.pallas_call(kernel, out_shape=jax.ShapeDtypeStruct((2, 128), F32), in_...  44.9 us
    unnamed x1, local copies, waits for them, and re-layouts  1.24 us

profile of v4, /device:TPU:1, one launch (start us, length us, event | category | flops | bytes accessed | tf_op | source)
XLA Modules:
  0.0 46.2 jit_solution(4102653646552798251)
XLA Ops:
  0.0 44.9 %shard_map.82 = f32[2,128]{1,0:T(2,128)} custom-call(bf16[2,512,512]{2,1,0:T(8,128)(2,1)} %sections.1, s32[2,2,2,2]{3,2,1,0:T(2,128)} %priors_h.1, s32[16]{0:T(128)} %row_order_h.1, bf16[512,512]{1,0:T(8,128)(2,1)} %constant.10.clone.table_h, bf16[512,512]{1,0:T(8,128)(2,1)} %constant.11.clone.table_t_h, f32[128,512]{1,0:T(8,128)} %constant.12.clone.lag_cos_h, ...), custom_call_target="tpu_custom_call" | custom-call | tf_op jit(solution)/shard_map/pallas_call | solution.py:504
  44.9 1.2 %copy.10 = f32[2,128]{1,0:T(2,128)} copy(f32[2,128]{1,0:T(2,128)} %shard_map.82) | data formatting | bytes 2048

commit v5 on v4

--- a/solution.py
+++ b/solution.py
@@ -283,6 +283,7 @@
         device_id=prior_id, device_id_type=MESH,
     )
 
+    prior_send.start()
     send(0, 0, 1)
     send(6, 0, 1)
     send(5, 0, 1)
@@ -292,7 +293,6 @@
     send(1, 2)
     send(10, 2)
     send(2, 0, 1, 2)
-    prior_send.start()
     for k in (10, 11):
         for down in range(2):
             send_row(k, down)
@@ -411,9 +411,8 @@
     rows_in(3)
     first_pass(p_buf, zpg.at[0], 2 * x_lo)
     edges(8)
-    pairs(0, x_lo)
     edges(9)
-    edges(4)
+    pairs(0, x_lo, lambda: edges(4))
     centre(10)
     centre(11)
     rows_in(6)

time: 46.3 us -> 43 us (0.929)
  Pallas kernels: 44.9 us -> 41.7 us
    pallas_call x1, Pallas kernels: 44.9 us -> 41.7 us  [body(): pl.pallas_call(kernel, out_shape=jax.ShapeDtypeStruct((2, 128), F32), in_...]
where the time goes in v5:
time: 43 us; the launch traced here: 42.9 us
  Pallas kernels  41.7 us (97%)
  local copies, waits for them, and re-layouts  1.24 us (3%)
    pallas_call x1, Pallas kernels, body(): pl.pallas_call(kernel, out_shape=jax.ShapeDtypeStruct((2, 128), F32), in_...  41.7 us
    unnamed x1, local copies, waits for them, and re-layouts  1.24 us

profile of v5, /device:TPU:1, one launch (start us, length us, event | category | flops | bytes accessed | tf_op | source)
XLA Modules:
  0.0 42.9 jit_solution(17386484890942926937)
XLA Ops:
  0.0 41.7 %shard_map.82 = f32[2,128]{1,0:T(2,128)} custom-call(bf16[2,512,512]{2,1,0:T(8,128)(2,1)} %sections.1, s32[2,2,2,2]{3,2,1,0:T(2,128)} %priors_h.1, s32[16]{0:T(128)} %row_order_h.1, bf16[512,512]{1,0:T(8,128)(2,1)} %constant.10.clone.table_h, bf16[512,512]{1,0:T(8,128)(2,1)} %constant.11.clone.table_t_h, f32[128,512]{1,0:T(8,128)} %constant.12.clone.lag_cos_h, ...), custom_call_target="tpu_custom_call" | custom-call | tf_op jit(solution)/shard_map/pallas_call | solution.py:503
  41.7 1.2 %copy.10 = f32[2,128]{1,0:T(2,128)} copy(f32[2,128]{1,0:T(2,128)} %shard_map.82) | data formatting | bytes 2048

commit v6 on v5

--- a/solution.py
+++ b/solution.py
@@ -287,12 +287,13 @@
     send(0, 0, 1)
     send(6, 0, 1)
     send(5, 0, 1)
-    send(0, 2)
     send(1, 0, 1)
+    send(2, 0, 1)
     send(5, 2)
     send(1, 2)
+    send(2, 2)
+    send(0, 2)
     send(10, 2)
-    send(2, 0, 1, 2)
     for k in (10, 11):
         for down in range(2):
             send_row(k, down)
@@ -371,48 +372,48 @@
     send(4, 0, 1, 2)
     tell(1)
     lag_tables_of(0)
-    edges(0, 7)
     rows_in(10)
     first_pass(m_buf, zm, 1 + 2 * x_lo)
-    centre(0, 7)
+    edges(0, 7)
+    rows_in(11)
+    first_pass(p_buf, zpg.at[0], 1)
     edges(5)
     edges(1, 8)
+    prior_send.wait_recv()
+    lag_tables_of(1)
+    edges(2)
     edges(7, 9)
     send(11, 2)
-    rows_in(11)
-    first_pass(p_buf, zpg.at[0], 1)
+    centre(5)
     centre(1, 8)
-    prior_send.wait_recv()
-    lag_tables_of(1)
-    centre(5)
-    rows_in(0, 5)
-    first_pass(m_buf, zm, 4 - 4 * x_lo)
-    centre(7, 9)
+    rows_in(1)
+    first_pass(m_buf, zm, 2)
     hear(1)
     tell(2)
-    rows_in(1)
-    first_pass(m_buf, zm, 2)
-    edges(2)
-    rows_in(7)
-    first_pass(m_buf, zm, 4 * x_lo)
     centre(2)
     rows_in(2)
     first_pass(p_buf, zpg.at[0], 2 - 2 * x_lo)
+
+    def arrivals():
+        centre(0, 7)
+        edges(3)
+
+    pairs(0, 1 - x_lo, arrivals)
+    edges(6)
+    rows_in(0, 5)
+    first_pass(m_buf, zm, 4 - 4 * x_lo)
     hear(2)
     tell(3)
-
-    def arrivals():
-        edges(3)
-        edges(6)
-
-    pairs(0, 1 - x_lo, arrivals)
-    hear(3)
+    centre(7, 9)
+    rows_in(7)
+    first_pass(m_buf, zm, 4 * x_lo)
+    edges(8)
+    edges(9)
     centre(3)
     rows_in(3)
     first_pass(p_buf, zpg.at[0], 2 * x_lo)
-    edges(8)
-    edges(9)
     pairs(0, x_lo, lambda: edges(4))
+    hear(3)
     centre(10)
     centre(11)
     rows_in(6)
@@ -457,14 +458,15 @@
 
     n_all = n_gz * n_row * n_col
     me = (gz * n_row + row) * n_col + col
-    for dg in range(n_gz):
-        for dr in range(n_row):
-            for dc in range(n_col):
-                if dg or dr or dc:
-                    pltpu.make_async_remote_copy(
-                        src_ref=flow_send, dst_ref=flow_recv.at[me], send_sem=send_f, recv_sem=recv_f,
-                        device_id=at(dg, dr, dc), device_id_type=MESH,
-                    ).start()
+    def hops(e):
+        return 2 * e[0] + min(e[1], n_row - e[1]) / 2 + min(e[2], n_col - e[2]) / 2
+
+    shifts = [(dg, dr, dc) for dg in range(n_gz) for dr in range(n_row) for dc in range(n_col) if dg or dr or dc]
+    for shift in sorted(shifts, key=hops, reverse=True):
+        pltpu.make_async_remote_copy(
+            src_ref=flow_send, dst_ref=flow_recv.at[me], send_sem=send_f, recv_sem=recv_f,
+            device_id=at(*shift), device_id_type=MESH,
+        ).start()
     want = [row_order[2 * row + m] for m in range(2)]
     picked = [jnp.zeros((1, 128), F32) for _ in range(2)]
     others = flow_recv.at[pl.ds(0, n_all - 1)]

time: 43 us -> 40.7 us (0.947)
  Pallas kernels: 41.7 us -> 39.3 us
    pallas_call x1, Pallas kernels: 41.7 us -> 39.3 us  [body(): pl.pallas_call(kernel, out_shape=jax.ShapeDtypeStruct((2, 128), F32), in_...]
where the time goes in v6:
time: 40.7 us; the launch traced here: 40.6 us
  Pallas kernels  39.3 us (97%)
  local copies, waits for them, and re-layouts  1.24 us (3%)
    pallas_call x1, Pallas kernels, body(): pl.pallas_call(kernel, out_shape=jax.ShapeDtypeStruct((2, 128), F32), in_...  39.3 us
    unnamed x1, local copies, waits for them, and re-layouts  1.24 us

profile of v6, /device:TPU:1, one launch (start us, length us, event | category | flops | bytes accessed | tf_op | source)
XLA Modules:
  0.0 40.6 jit_solution(11934727075690702199)
XLA Ops:
  0.0 39.3 %shard_map.82 = f32[2,128]{1,0:T(2,128)} custom-call(bf16[2,512,512]{2,1,0:T(8,128)(2,1)} %sections.1, s32[2,2,2,2]{3,2,1,0:T(2,128)} %priors_h.1, s32[16]{0:T(128)} %row_order_h.1, bf16[512,512]{1,0:T(8,128)(2,1)} %constant.10.clone.table_h, bf16[512,512]{1,0:T(8,128)(2,1)} %constant.11.clone.table_t_h, f32[128,512]{1,0:T(8,128)} %constant.12.clone.lag_cos_h, ...), custom_call_target="tpu_custom_call" | custom-call | tf_op jit(solution)/shard_map/pallas_call | solution.py:505
  39.3 1.2 %copy.10 = f32[2,128]{1,0:T(2,128)} copy(f32[2,128]{1,0:T(2,128)} %shard_map.82) | data formatting | bytes 2048

commit v7 on v6

--- a/solution.py
+++ b/solution.py
@@ -119,6 +119,16 @@
     body = pl.ds(128, 512)
     p_buf, g_buf = pg_buf.at[0], pg_buf.at[1]
 
+    def at(dg, dr, dc):
+        return (lax.rem(gz + dg, n_gz), lax.rem(row + dr, n_row), lax.rem(col + dc, n_col))
+
+    z_ring = [at(0, 0, 2), at(0, 0, n_col - 2)]
+    row_ring = [at(0, 1, 0), at(0, n_row - 1, 0)]
+    near_peers = [a_id, b_id] + z_ring + row_ring
+    barrier = pltpu.get_barrier_semaphore()
+    for peer in near_peers:
+        pl.semaphore_signal(barrier, inc=1, device_id=peer, device_id_type=MESH)
+
     own_m = pltpu.make_async_copy(sections.at[x_lo], m_buf.at[body, pl.ds(c0, 512)], local_sem.at[0])
     own_p = pltpu.make_async_copy(sections.at[1 - x_lo], p_buf.at[body, pl.ds(128, 512)], local_sem.at[1])
     own_m.start()
@@ -132,16 +142,6 @@
     ]
     for copy in constants:
         copy.start()
-
-    def at(dg, dr, dc):
-        return (lax.rem(gz + dg, n_gz), lax.rem(row + dr, n_row), lax.rem(col + dc, n_col))
-
-    z_ring = [at(0, 0, 2), at(0, 0, n_col - 2)]
-    row_ring = [at(0, 1, 0), at(0, n_row - 1, 0)]
-    near_peers = [a_id, b_id] + z_ring + row_ring
-    barrier = pltpu.get_barrier_semaphore()
-    for peer in near_peers:
-        pl.semaphore_signal(barrier, inc=1, device_id=peer, device_id_type=MESH)
 
     rounds = [
         near_peers,
@@ -293,7 +293,6 @@
     send(1, 2)
     send(2, 2)
     send(0, 2)
-    send(10, 2)
     for k in (10, 11):
         for down in range(2):
             send_row(k, down)
@@ -372,18 +371,19 @@
     send(4, 0, 1, 2)
     tell(1)
     lag_tables_of(0)
+    edges(0, 7)
     rows_in(10)
     first_pass(m_buf, zm, 1 + 2 * x_lo)
-    edges(0, 7)
+    edges(1, 8)
+    send(10, 2)
+    edges(2)
+    edges(7, 9)
+    send(11, 2)
     rows_in(11)
     first_pass(p_buf, zpg.at[0], 1)
     edges(5)
-    edges(1, 8)
     prior_send.wait_recv()
     lag_tables_of(1)
-    edges(2)
-    edges(7, 9)
-    send(11, 2)
     centre(5)
     centre(1, 8)
     rows_in(1)

time: 40.7 us -> 40.7 us (level)
  no operation moved by 1% of the time
where the time goes in v7:
time: 40.7 us; the launch traced here: 40.6 us
  Pallas kernels  39.3 us (97%)
  local copies, waits for them, and re-layouts  1.24 us (3%)
    pallas_call x1, Pallas kernels, body(): pl.pallas_call(kernel, out_shape=jax.ShapeDtypeStruct((2, 128), F32), in_...  39.3 us
    unnamed x1, local copies, waits for them, and re-layouts  1.24 us

profile of v7, /device:TPU:1, one launch (start us, length us, event | category | flops | bytes accessed | tf_op | source)
XLA Modules:
  0.0 40.6 jit_solution(13900498511844947156)
XLA Ops:
  0.0 39.3 %shard_map.82 = f32[2,128]{1,0:T(2,128)} custom-call(bf16[2,512,512]{2,1,0:T(8,128)(2,1)} %sections.1, s32[2,2,2,2]{3,2,1,0:T(2,128)} %priors_h.1, s32[16]{0:T(128)} %row_order_h.1, bf16[512,512]{1,0:T(8,128)(2,1)} %constant.10.clone.table_h, bf16[512,512]{1,0:T(8,128)(2,1)} %constant.11.clone.table_t_h, f32[128,512]{1,0:T(8,128)} %constant.12.clone.lag_cos_h, ...), custom_call_target="tpu_custom_call" | custom-call | tf_op jit(solution)/shard_map/pallas_call | solution.py:505
  39.3 1.2 %copy.10 = f32[2,128]{1,0:T(2,128)} copy(f32[2,128]{1,0:T(2,128)} %shard_map.82) | data formatting | bytes 2048
